TPU v7x, 16 devices: a 4x2x1 block of a 4x4x8 slice. The times are simulated.
16 devices in a mesh: rep: 4 (over y, z, core), dp: 4 (over x).
Axes of the slice: x: 4, y: 2, z: 1, core: 2. Of those that a mesh axis runs over, the one named last changes fastest.
The devices are a block of a 4x4x8 slice.
Arguments:
- x: bfloat16 [16, 1024, 1024], P(('rep', 'dp')), parts along dimension 0
- dy: bfloat16 [16, 1024, 1024], P(('rep', 'dp')), parts along dimension 0
- w_gate: bfloat16 [2, 1024, 3200], replicated
- w_up: bfloat16 [2, 1024, 3200], replicated
- w_down: bfloat16 [2, 3200, 1024], replicated
- m_w_gate: float32 [2, 1024, 3200], replicated
- m_w_up: float32 [2, 1024, 3200], replicated
- m_w_down: float32 [2, 3200, 1024], replicated
- v_w_gate: float32 [2, 1024, 3200], replicated
- v_w_up: float32 [2, 1024, 3200], replicated
- v_w_down: float32 [2, 3200, 1024], replicated
Outputs:
- output 1: bfloat16 [8, 1024, 3200], P('rep'), parts along dimension 0
- output 2: bfloat16 [8, 1024, 3200], P('rep'), parts along dimension 0
- output 3: bfloat16 [8, 3200, 1024], P('rep'), parts along dimension 0
- output 4: float32 [8, 1024, 3200], P('rep'), parts along dimension 0
- output 5: float32 [8, 1024, 3200], P('rep'), parts along dimension 0
- output 6: float32 [8, 3200, 1024], P('rep'), parts along dimension 0
- output 7: float32 [8, 1024, 3200], P('rep'), parts along dimension 0
- output 8: float32 [8, 1024, 3200], P('rep'), parts along dimension 0
- output 9: float32 [8, 3200, 1024], P('rep'), parts along dimension 0
There are 4 independent parts. A program takes and returns all parts, laid end to end along the dimension named above; an argument that names none is the same for every part.
All inputs are finite; a program needn't handle non-finite values.
Results may differ from a plain program's by a relative error of at most 0.022.
Values are sent between devices in bfloat16 or wider.
A program may use at most 768 MiB of HBM per device.

v0:
```python
import jax
import jax.numpy as jnp
from jax import lax
from jax.sharding import PartitionSpec as P

NAMES = ("w_gate", "w_up", "w_down")


def matmul(a, w):
    return jnp.dot(a, w, preferred_element_type=jnp.float32).astype(jnp.bfloat16)


def normed(h):
    wide = h.astype(jnp.float32)
    scale = lax.rsqrt(jnp.mean(wide**2, -1, keepdims=True) + 1e-6)
    return (wide * scale).astype(jnp.bfloat16)


def layer(h, w):
    a = normed(h)
    gate = jnp.dot(a, w["w_gate"], preferred_element_type=jnp.float32)
    up = jnp.dot(a, w["w_up"], preferred_element_type=jnp.float32)
    return h + matmul((jax.nn.silu(gate) * up).astype(jnp.bfloat16), w["w_down"])


def adamw(w, m, v, g):
    m = 0.9 * m + 0.1 * g
    v = 0.95 * v + 0.05 * g * g
    step = m * lax.rsqrt(v + 1e-8) + 0.1 * w
    return (w - 0.02 * step).astype(jnp.bfloat16), m, v


def clipped(gradients, sum_of_squares, count):
    factor = jnp.minimum(1.0, 0.5 * lax.rsqrt(sum_of_squares / count + 1e-30))
    return [g * factor for g in gradients]


def solution(mesh):
    def step(x, dy, *arrays):
        weights, m, v = (arrays[i : i + 3] for i in (0, 3, 6))
        layers = weights[0].shape[0]
        h, kept = x[0], []
        for number in range(layers):
            kept.append(h)
            h = layer(h, {name: w[number] for name, w in zip(NAMES, weights, strict=True)})
        by_h, summed = dy[0], [None] * layers
        for number in reversed(range(layers)):
            _, back = jax.vjp(lambda w, h: layer(h, w), {name: w[number] for name, w in zip(NAMES, weights, strict=True)}, kept[number])
            by_w, by_h = back(by_h)
            summed[number] = [lax.psum(by_w[name], "dp") for name in NAMES]
        gradients = [jnp.stack([summed[number][i] for number in range(layers)]).astype(jnp.float32) for i in range(3)]
        gradients = clipped(gradients, sum(jnp.sum(g * g) for g in gradients), sum(g.size for g in gradients))
        new = [adamw(w.astype(jnp.float32), m, v, g) for w, m, v, g in zip(weights, m, v, gradients, strict=True)]
        return tuple(one[which] for which in range(3) for one in new)

    return jax.shard_map(
        step,
        mesh=mesh,
        in_specs=(P(("rep", "dp"), None, None),) * 2 + (P(None, None, None),) * 9,
        out_specs=(P("rep", None, None),) * 9,
        check_vma=False,
    )
```

profile of v0, /device:TPU:112, one launch (start us, length us, event | category | flops | bytes accessed | tf_op | source)
XLA Modules:
  0.0 1063.4 jit_solution(12048922128296325136)
XLA Ops:
  7.3 2.9 copy.20
  10.6 4.2 copy.21
  14.8 12.5 %convolution_convert_fusion.4 = bf16[1024,3200]{1,0:T(8,128)(2,1)} fusion(bf16[2,3200,1024]{2,1,0:T(8,128)(2,1)} %param.15, bf16[1,1024,1024]{2,1,0:T(8,128)(2,1)} %param.12), kind=kOutput, calls=%fused_computation.68 | convolution fusion | flops 6714163200 | bytes 15204352 | tf_op jit(solution)/shard_map/transpose(jvp())/dot_general | solution.py:10
  27.4 10.5 fusion.52
  37.9 16.7 %multiply_convert_fusion.1 = (bf16[1024,3200]{1,0:T(8,128)(2,1)}, f32[1024,3200]{1,0:T(8,128)}) fusion(f32[1024,3200]{1,0:T(8,128)} %fusion.52, bf16[2,1024,3200]{2,1,0:T(8,128)(2,1)} %param.14, bf16[1,1024,1024]{2,1,0:T(8,128)(2,1)} %param.11, f32[1024]{0:T(1024)S(1)} %add_rsqrt_fusion), kind=kOutput, calls=%fused_computation.56 | convolution fusion | flops 6733692928 | bytes 41422848 | tf_op jit(solution)/shard_map/dot_general | solution.py:22
  54.6 11.6 %fusion.76 = (f32[1024]{0:T(1024)S(1)}, bf16[1024,1024]{0,1:T(8,128)(2,1)S(1)}) fusion(bf16[1024,3200]{1,0:T(8,128)(2,1)} %get-tuple-element.24, bf16[2,3200,1024]{2,1,0:T(8,128)(2,1)} %param.15, bf16[1,1024,1024]{1,2,0:T(8,128)(2,1)S(1)} %copy.20), kind=kOutput, calls=%fused_computation.111 | convolution fusion | flops 6716128256 | bytes 17305600 | tf_op jit(solution)/shard_map/dot_general | solution.py:10
  67.5 13.2 %fusion.39 = f32[1024,3200]{1,0:T(8,128)} fusion(bf16[2,1024,3200]{2,1,0:T(8,128)(2,1)} %param.14, bf16[1024,1024]{0,1:T(8,128)(2,1)S(1)} %get-tuple-element.27, f32[1024]{0:T(1024)S(1)} %fusion.96), kind=kOutput, calls=%fused_computation.73 | convolution fusion | flops 6714032128 | bytes 21762048 | tf_op jit(solution)/shard_map/jvp()/dot_general | solution.py:22
  80.8 23.4 %fusion.23 = (bf16[1024,3200]{1,0:T(8,128)(2,1)}, f32[1024,3200]{1,0:T(8,128)}) fusion(f32[1024,3200]{1,0:T(8,128)} %fusion.39, bf16[1024,3200]{1,0:T(8,128)(2,1)} %convolution_convert_fusion.4, bf16[2,1024,3200]{2,1,0:T(8,128)(2,1)} %param.13, bf16[1024,1024]{0,1:T(8,128)(2,1)} %copy-done.3, f32[1024]{0:T(1024)S(1)} %fusion.96), kind=kOutput, calls=%fused_computation.44 | convolution fusion | flops 6753353728 | bytes 47976448 | tf_op jit(solution)/shard_map/jvp()/dot_general | solution.py:21
  104.2 13.5 %fusion.33 = bf16[1024,1024]{0,1:T(8,128)(2,1)S(1)} fusion(bf16[1024,3200]{1,0:T(8,128)(2,1)} %convolution_convert_fusion.4, bf16[2,1024,3200]{2,1,0:T(8,128)(2,1)} %param.14, f32[1024,3200]{1,0:T(8,128)} %get-tuple-element.29), kind=kOutput, calls=%fused_computation.60 | convolution fusion | flops 6730547200 | bytes 28311552 | tf_op jit(solution)/shard_map/transpose(jvp())/dot_general | solution.py:22
  117.7 14.6 %fusion.65 = bf16[1,1024,3200]{2,1,0:T(8,128)(2,1)} fusion(bf16[1024,3200]{1,0:T(8,128)(2,1)} %convolution_convert_fusion.4, bf16[1024,1024]{0,1:T(8,128)(2,1)S(1)} %copy-done.4, f32[1024]{0:T(1024)S(1)} %fusion.96, f32[1024,3200]{1,0:T(8,128)} %get-tuple-element.29), kind=kOutput, calls=%fused_computation.97 | convolution fusion | flops 6736969728 | bytes 28315648 | tf_op jit(solution)/shard_map/transpose(jvp())/dot_general | solution.py:22
  132.4 14.7 %fusion.60 = bf16[1,3200,1024]{2,1,0:T(8,128)(2,1)} fusion(f32[1024,3200]{1,0:T(8,128)} %fusion.39, bf16[1,1024,1024]{2,1,0:T(8,128)(2,1)S(1)} %copy-done.6, f32[1024,3200]{1,0:T(8,128)} %get-tuple-element.29), kind=kOutput, calls=%fused_computation.94 | convolution fusion | flops 6733824000 | bytes 34865152 | tf_op jit(solution)/shard_map/transpose(jvp())/dot_general | solution.py:10
  147.1 12.1 %fusion.58 = bf16[1,1024,3200]{2,1,0:T(8,128)(2,1)} fusion(bf16[1024,3200]{1,0:T(8,128)(2,1)} %get-tuple-element.28, bf16[1024,1024]{0,1:T(8,128)(2,1)S(1)} %copy-done.4, f32[1024]{0:T(1024)S(1)} %fusion.96), kind=kOutput, calls=%fused_computation.92 | convolution fusion | flops 6714032128 | bytes 15208448 | tf_op jit(solution)/shard_map/transpose(jvp())/dot_general | solution.py:21
  159.1 11.8 %fusion.78 = (f32[1024]{0:T(1024)S(1)}, bf16[1024,1024]{0,1:T(8,128)(2,1)S(1)}) fusion(bf16[1024,1024]{0,1:T(8,128)(2,1)S(1)} %copy-done.4, bf16[1024,1024]{0,1:T(8,128)(2,1)S(1)} %fusion.33, bf16[1024,3200]{1,0:T(8,128)(2,1)} %get-tuple-element.28, bf16[2,1024,3200]{2,1,0:T(8,128)(2,1)} %param.13), kind=kOutput, calls=%fused_computation.113 | convolution fusion | flops 6716128256 | bytes 19402752 | tf_op jit(solution)/shard_map/transpose(jvp())/dot_general | solution.py:21
  171.0 1.6 fusion.81
  172.6 9.3 convolution_convert_fusion.3
  182.0 12.0 %fusion.59 = bf16[1,3200,1024]{2,1,0:T(8,128)(2,1)} fusion(bf16[1024,3200]{1,0:T(8,128)(2,1)} %get-tuple-element.24, bf16[1024,1024]{0,1:T(8,128)(2,1)S(1)} %fusion.81), kind=kOutput, calls=%fused_computation.93 | convolution fusion | flops 6714163200 | bytes 15204352 | tf_op jit(solution)/shard_map/transpose(jvp())/dot_general | solution.py:10
  194.0 13.3 %fusion.61 = bf16[1,1024,3200]{2,1,0:T(8,128)(2,1)} fusion(bf16[1024,3200]{1,0:T(8,128)(2,1)S(1)} %copy-done.11, f32[1024,3200]{1,0:T(8,128)} %fusion.52, bf16[1,1024,1024]{1,2,0:T(8,128)(2,1)S(1)} %copy-done.2, f32[1024]{0:T(1024)S(1)} %copy-done.10), kind=kOutput, calls=%fused_computation.95 | convolution fusion | flops 6736969728 | bytes 28315648 | tf_op jit(solution)/shard_map/transpose(jvp())/dot_general | solution.py:22
  207.3 16.9 %fusion.62 = bf16[1,1024,3200]{2,1,0:T(8,128)(2,1)} fusion(f32[1024,3200]{1,0:T(8,128)} %fusion.52, f32[1024,3200]{1,0:T(8,128)} %get-tuple-element.25, bf16[1024,3200]{1,0:T(8,128)(2,1)} %convolution_convert_fusion.3, bf16[1,1024,1024]{1,2,0:T(8,128)(2,1)S(1)} %copy-done.2, f32[1024]{0:T(1024)S(1)} %copy-done.10), kind=kOutput, calls=%fused_computation.96 | convolution fusion | flops 6753353728 | bytes 41422848 | tf_op jit(solution)/shard_map/transpose(jvp())/dot_general | solution.py:21
  224.3 652.6 %all-reduce.3.cloned.1.call-done = (bf16[1,1024,3200]{2,1,0:T(8,128)(2,1)}, bf16[1,1024,3200]{2,1,0:T(8,128)(2,1)}, bf16[1,1024,3200]{2,1,0:T(8,128)(2,1)}, bf16...) async-done(((bf16[1,1024,3200]{2,1,0:T(8,128)(2,1)}, bf16[1,1024,3200]{2,1,0:T(8,128)(2,1)}, ...) | async-done | bytes 39321616 | tf_op jit(solution)/shard_map/psum | solution.py:50
  876.9 12.1 %fusion.9 = f32[]{:T(128)} fusion(bf16[1,1024,3200]{2,1,0:T(8,128)(2,1)} %get-tuple-element.9, bf16[1,1024,3200]{2,1,0:T(8,128)(2,1)} %get-tuple-element.10), kind=kLoop, calls=%fused_computation.24 | loop fusion | flops 26214400 | bytes 13107204 | tf_op jit(solution)/shard_map/reduce_sum | solution.py:52
  889.0 12.1 %fusion.10 = f32[]{:T(128)} fusion(bf16[1,1024,3200]{2,1,0:T(8,128)(2,1)} %get-tuple-element.11, bf16[1,1024,3200]{2,1,0:T(8,128)(2,1)} %get-tuple-element.12), kind=kLoop, calls=%fused_computation.25 | loop fusion | flops 26214400 | bytes 13107204 | tf_op jit(solution)/shard_map/reduce_sum | solution.py:52
  902.4 12.2 %fusion.11 = f32[]{:T(128)} fusion(bf16[1,3200,1024]{2,1,0:T(8,128)(2,1)} %get-tuple-element.13, bf16[1,3200,1024]{2,1,0:T(8,128)(2,1)} %get-tuple-element.14), kind=kLoop, calls=%fused_computation.26 | loop fusion | flops 26214400 | bytes 13107204 | tf_op jit(solution)/shard_map/reduce_sum | solution.py:52
  915.3 49.8 %fusion.17 = (bf16[2,3200,1024]{2,1,0:T(8,128)(2,1)}, f32[2,3200,1024]{2,1,0:T(8,128)}, f32[2,3200,1024]{2,1,0:T(8,128)}) fusion(bf16[2,3200,1024]{2,1,0:T(8,128)(2,1)} %param.15, f32[]{:T(128)S(6)} %min_shard_map.3, bf16[1,3200,1024]{2,1,0:T(8,128)(2,1)} %get-tuple-element.13, bf16[1,3200,1024]{2,1,0:T(8,128)(2,1)} %get-tuple-element.14, ...), kind=kLoop, calls=%fused_computation.32 | loop fusion | flops 131072000 | bytes 144179200 | tf_op jit(solution)/shard_map/convert_element_type | solution.py:30
  965.1 91.3 %fusion.8 = (bf16[2,1024,3200]{2,1,0:T(8,128)(2,1)}, f32[2,1024,3200]{2,1,0:T(8,128)}, f32[2,1024,3200]{2,1,0:T(8,128)}, bf16[2,1024,3200]{2,1,0:T(8,128)(2,1)},...) fusion(bf16[2,1024,3200]{2,1,0:T(8,128)(2,1)} %param.13, f32[]{:T(128)S(6)} %min_shard_map.3, ...), kind=kLoop, calls=%fused_computation.23 | loop fusion | flops 262144000 | bytes 288358400 | tf_op jit(solution)/shard_map/convert_element_type | solution.py:30
  (48 shorter events, 2.0 us)
Async XLA Ops:
  7.2 869.7 %all-reduce.3.cloned.1.call-start = ((), (), s32[]{:S(2)}) async-start(), calls=%async_computation | async-start | bytes 78643200 | tf_op jit(solution)/shard_map/psum | solution.py:50
  10.1 44.5 %copy-start.1 = (bf16[1,1024,1024]{1,2,0:T(8,128)(2,1)}, bf16[1,1024,1024]{1,2,0:T(8,128)(2,1)S(1)}, u32[]{:S(2)}) copy-start(bf16[1,1024,1024]{1,2,0:T(8,128)(2,1)S(1)} %copy.20) | copy-start | bytes 6291460
  10.6 27.2 %copy-start.9 = (f32[1024]{0:T(1024)}, f32[1024]{0:T(1024)S(1)}, u32[]{:S(2)}) copy-start(f32[1024]{0:T(1024)S(1)} %add_rsqrt_fusion) | copy-start | bytes 12292
  10.6 16.7 %slice-start.4 = ((s8[13107200]{0:T(1024)(128)(4,1)}), s8[524288]{0:T(1024)(128)(4,1)S(1)}, s32[]{:S(2)}) async-start(s8[13107200]{0:T(1024)(128)(4,1)} %bitcast.76), calls=%async_computation.5 | async-start | bytes 1048576
  14.8 12.5 %slice-start.5 = ((s8[13107200]{0:T(1024)(128)(4,1)}), s8[4194304]{0:T(1024)(128)(4,1)S(1)}, s32[]{:S(2)}) async-start(s8[13107200]{0:T(1024)(128)(4,1)} %bitcast.76), calls=%async_computation.6 | async-start | bytes 8388608
  14.8 12.5 %slice-start.6 = ((s8[13107200]{0:T(1024)(128)(4,1)}), s8[4194304]{0:T(1024)(128)(4,1)S(1)}, s32[]{:S(2)}) async-start(s8[13107200]{0:T(1024)(128)(4,1)} %bitcast.76), calls=%async_computation.7 | async-start | bytes 8388608
  14.8 12.5 %slice-start.7 = ((s8[13107200]{0:T(1024)(128)(4,1)}), s8[4194304]{0:T(1024)(128)(4,1)S(1)}, s32[]{:S(2)}) async-start(s8[13107200]{0:T(1024)(128)(4,1)} %bitcast.76), calls=%async_computation.8 | async-start | bytes 8388608
  14.8 12.5 %copy-start.5 = (bf16[1,1024,1024]{2,1,0:T(8,128)(2,1)S(1)}, bf16[1,1024,1024]{2,1,0:T(8,128)(2,1)}, u32[]{:S(2)}) copy-start(bf16[1,1024,1024]{2,1,0:T(8,128)(2,1)} %param.11) | copy-start | bytes 6291460
  66.2 1.3 copy-start.3
  66.2 38.0 %copy-start.7 = (f32[1024]{0:T(1024)}, f32[1024]{0:T(1024)S(1)}, u32[]{:S(2)}) copy-start(f32[1024]{0:T(1024)S(1)} %get-tuple-element.26) | copy-start | bytes 12292
  104.2 13.5 %copy-start.4 = (bf16[1024,1024]{0,1:T(8,128)(2,1)S(1)}, bf16[1024,1024]{0,1:T(8,128)(2,1)}, u32[]{:S(2)}) copy-start(bf16[1024,1024]{0,1:T(8,128)(2,1)} %copy-done.3) | copy-start | bytes 6291460
  117.7 14.7 %copy-start.6 = (bf16[1,1024,1024]{2,1,0:T(8,128)(2,1)S(1)}, bf16[1,1024,1024]{2,1,0:T(8,128)(2,1)}, u32[]{:S(2)}) copy-start(bf16[1,1024,1024]{2,1,0:T(8,128)(2,1)} %param.12) | copy-start | bytes 6291460
  147.1 25.5 %slice-start = ((s8[13107200]{0:T(1024)(128)(4,1)}), s8[4194304]{0:T(1024)(128)(4,1)S(1)}, s32[]{:S(2)}) async-start(s8[13107200]{0:T(1024)(128)(4,1)} %bitcast.74), calls=%async_computation.1 | async-start | bytes 8388608
  147.1 25.5 %slice-start.1 = ((s8[13107200]{0:T(1024)(128)(4,1)}), s8[4194304]{0:T(1024)(128)(4,1)S(1)}, s32[]{:S(2)}) async-start(s8[13107200]{0:T(1024)(128)(4,1)} %bitcast.74), calls=%async_computation.2 | async-start | bytes 8388608
  147.1 25.6 %slice-start.2 = ((s8[13107200]{0:T(1024)(128)(4,1)}), s8[4194304]{0:T(1024)(128)(4,1)S(1)}, s32[]{:S(2)}) async-start(s8[13107200]{0:T(1024)(128)(4,1)} %bitcast.74), calls=%async_computation.3 | async-start | bytes 8388608
  159.1 11.9 %copy-start.8 = (f32[1024]{0:T(1024)S(1)}, f32[1024]{0:T(1024)}, u32[]{:S(2)}) copy-start(f32[1024]{0:T(1024)} %copy-done.7) | copy-start | bytes 12292
  159.1 11.9 %copy-start = (bf16[1,1024,1024]{1,2,0:T(8,128)(2,1)S(1)}, bf16[1,1024,1024]{1,2,0:T(8,128)(2,1)}, u32[]{:S(2)}) copy-start(bf16[1,1024,1024]{1,2,0:T(8,128)(2,1)} %copy.21) | copy-start | bytes 6291460
  159.1 13.5 %slice-start.3 = ((s8[13107200]{0:T(1024)(128)(4,1)}), s8[524288]{0:T(1024)(128)(4,1)S(1)}, s32[]{:S(2)}) async-start(s8[13107200]{0:T(1024)(128)(4,1)} %bitcast.74), calls=%async_computation.4 | async-start | bytes 1048576
  182.0 12.0 %copy-start.2 = (bf16[1,1024,1024]{1,2,0:T(8,128)(2,1)S(1)}, bf16[1,1024,1024]{1,2,0:T(8,128)(2,1)}, u32[]{:S(2)}) copy-start(bf16[1,1024,1024]{1,2,0:T(8,128)(2,1)} %copy-done.1) | copy-start | bytes 6291460
  182.0 12.0 %copy-start.10 = (f32[1024]{0:T(1024)S(1)}, f32[1024]{0:T(1024)}, u32[]{:S(2)}) copy-start(f32[1024]{0:T(1024)} %copy-done.9) | copy-start | bytes 12292
  182.0 12.0 %copy-start.11 = (bf16[1024,3200]{1,0:T(8,128)(2,1)S(1)}, bf16[1024,3200]{1,0:T(8,128)(2,1)}, u32[]{:S(2)}) copy-start(bf16[1024,3200]{1,0:T(8,128)(2,1)} %convolution_convert_fusion.3) | copy-start | bytes 19660804
Sparse Core Ops, SparseCore 0:
  224.4 652.4 all-reduce.2
where the time goes:
time: 1070 us; the launch traced here: 1060 us
  waiting for transfers between devices  653 us (61%)
  matrix products  206 us (19%)
  other arithmetic  180 us (17%)
  between operations  16.5 us (2%)
    psum x1, waiting for transfers between devices, step(): summed[number] = [lax.psum(by_w[name], 'dp') for name in NAMES]  653 us
    convert_element_type x2, other arithmetic, adamw(): return ((w - 0.02 * step).astype(jnp.bfloat16), m, v)  141 us
    dot_general x5, matrix products, layer(): gate = jnp.dot(a, w['w_gate'], preferred_element_type=jnp.float32)  74.7 us
    dot_general x5, matrix products, layer(): up = jnp.dot(a, w['w_up'], preferred_element_type=jnp.float32)  71.4 us
    dot_general x5, matrix products, matmul(): jnp.dot(a, w, preferred_element_type=jnp.float32).astype(jnp.bfloat16)  60.2 us
    reduce_sum x3, other arithmetic, step(): jnp.sum(g * g)  36.4 us
  transfers between devices with their start and end apart: 1, of which 1 were waited for; matrix products, arithmetic and copies ran while one was open for 0% of the time, Pallas kernels for 0%

commit v1 on v0

v1 whole, which is shorter than its diff:
```python
import functools

import jax
import jax.numpy as jnp
from jax import lax
from jax.experimental import pallas as pl
from jax.experimental.pallas import tpu as pltpu
from jax.sharding import PartitionSpec as P

F32, BF16 = jnp.float32, jnp.bfloat16
LANES = 128
STEPS = 8


def normed(h):
    wide = h.astype(F32)
    scale = lax.rsqrt(jnp.mean(wide**2, -1, keepdims=True) + 1e-6)
    return (wide * scale).astype(BF16)


def dot(a, b, da=1, db=0):
    return lax.dot_general(a, b, (((da,), (db,)), ((), ())), preferred_element_type=F32)


def gated(a, dout, w_gate, w_up, w_down):
    gate, up = dot(a, w_gate), dot(a, w_up)
    by_hidden = dot(dout, w_down, 1, 1).astype(BF16).astype(F32)
    s = jax.nn.sigmoid(gate)
    silu = gate * s
    hidden = (silu * up).astype(BF16)
    by_up = (by_hidden * silu).astype(BF16)
    by_gate = (by_hidden * up * (s * (1 + gate * (1 - s)))).astype(BF16)
    return hidden, by_gate, by_up


def adamw_kernel(at, factor, *refs):
    del at
    grads, w, m, v = (refs[i : i + 3] for i in (0, 3, 6, 9))
    w_out, m_out, v_out = (refs[len(refs) - 9 + i : len(refs) - 6 + i] for i in (0, 3, 6))
    c = factor[0]
    for i in range(3):
        g = grads[i][...].astype(F32) * c
        mm = 0.9 * m[i][0] + 0.1 * g
        vv = 0.95 * v[i][0] + 0.05 * g * g
        wide = w[i][0].astype(F32)
        step = mm * lax.rsqrt(vv + 1e-8) + 0.1 * wide
        w_out[i][0] = (wide - 0.02 * step).astype(BF16)
        m_out[i][0] = mm
        v_out[i][0] = vv


def adamw(layer, block, factor, grads, weights, m, v, so_far):
    d, width = grads[0].shape
    at = jnp.stack([jnp.int32(layer), jnp.asarray(block, jnp.int32)])
    rows, down_rows = d // STEPS, width // STEPS
    by_column = pl.BlockSpec((rows, width), lambda i, at, f: (i, 0))
    by_row = pl.BlockSpec((down_rows, d), lambda i, at, f: (i, 0))
    column = pl.BlockSpec((1, rows, width), lambda i, at, f: (at[0], i, at[1]))
    row = pl.BlockSpec((1, down_rows, d), lambda i, at, f: (at[0], at[1] * STEPS + i, 0))
    whole = [column, column, row]
    shapes = [jax.ShapeDtypeStruct(a.shape, t) for t in (BF16, F32, F32) for a in weights]
    olds = () if so_far is None else tuple(so_far)
    elements = 3 * d * width
    return pl.pallas_call(
        adamw_kernel,
        grid_spec=pltpu.PrefetchScalarGridSpec(
            num_scalar_prefetch=2,
            grid=(STEPS,),
            in_specs=[by_column, by_column, by_row] + whole * 3 + [pl.BlockSpec(memory_space=pl.ANY)] * len(olds),
            out_specs=whole * 3,
        ),
        out_shape=shapes,
        input_output_aliases={14 + i: i for i in range(len(olds))},
        compiler_params=pltpu.CompilerParams(dimension_semantics=("arbitrary",), vmem_limit_bytes=40 * 2**20),
        cost_estimate=pl.CostEstimate(flops=elements * 900, bytes_accessed=elements * 22, transcendentals=elements),
        name="adamw",
    )(at, factor, *grads, *weights, *m, *v, *olds)


def solution(mesh):
    n = mesh.shape["dp"]
    right = [(i, (i + 1) % n) for i in range(n)]
    left = [(i, (i - 1) % n) for i in range(n)]

    def around(block):
        half = block.shape[0] // 2
        before, after = lax.ppermute(block, "dp", right), lax.ppermute(block, "dp", left)
        top, bottom = lax.ppermute(before[:half], "dp", right), lax.ppermute(after[half:], "dp", left)
        return before, after, jnp.concatenate([top, bottom])

    def gathered(block):
        me = lax.axis_index("dp")
        before, after, far = around(block)
        every = jnp.zeros((n, *block.shape), block.dtype)
        for away, part in ((0, block), (n - 1, before), (1, after), (2, far)):
            every = lax.dynamic_update_slice(every, part[None], ((me + away) % n, 0, 0))
        return every.reshape(n * block.shape[0], block.shape[1])

    def step(x, dy, *arrays):
        weights, m, v = (arrays[i : i + 3] for i in (0, 3, 6))
        w_gate, w_up, w_down = weights
        layers, d, ff = w_gate.shape
        assert n == 4 and layers == 2
        own = ff // (n + 1) // LANES * LANES
        assert own * (n + 1) == ff
        me = lax.axis_index("dp")
        x, dy = x[0], dy[0]

        dy_all = gathered(dy)
        a = normed(x)
        hidden = (jax.nn.silu(dot(a, w_gate[0])) * dot(a, w_up[0])).astype(BF16)
        h = x + dot(hidden, w_down[0]).astype(BF16)
        h_all = gathered(h)
        a, back = jax.vjp(normed, h)
        _, by_gate, by_up = gated(a, dy, w_gate[1], w_up[1], w_down[1])
        by_a = (dot(by_gate, w_gate[1], 1, 1) + dot(by_up, w_up[1], 1, 1)).astype(BF16)
        by_h = dy + back(by_a)[0]
        x_all = gathered(x)
        by_h_all = gathered(by_h)

        def units(w, axis):
            return jnp.concatenate([lax.dynamic_slice_in_dim(w, me * own, own, axis), lax.slice_in_dim(w, n * own, ff, axis=axis)], axis)

        grads = [None] * layers
        squares, common = jnp.float32(0), jnp.float32(0)
        for number, (inputs, outs) in reversed(list(enumerate(((x_all, by_h_all), (h_all, dy_all))))):
            a = normed(inputs)
            hidden, by_gate, by_up = gated(a, outs, units(w_gate[number], 1), units(w_up[number], 1), units(w_down[number], 0))
            down = dot(hidden, outs, 0, 0).astype(BF16)
            gate, up = dot(a, by_gate, 0, 0).astype(BF16), dot(a, by_up, 0, 0).astype(BF16)
            mine = (gate[:, :own], up[:, :own], down[:own])
            shared = (gate[:, own:], up[:, own:], down[own:])
            squares += sum(jnp.sum(g.astype(F32) ** 2) for g in mine)
            common += sum(jnp.sum(g.astype(F32) ** 2) for g in shared)
            others = [around(g) for g in mine]
            grads[number] = [(me, mine), (n, shared)] + [
                ((me + away) % n, tuple(o[i] for o in others)) for i, away in enumerate((n - 1, 1, 2))
            ]
        count = sum(w.size for w in weights)
        total = lax.psum(squares, "dp") + common
        factor = jnp.minimum(1.0, 0.5 * lax.rsqrt(total / count + 1e-30)).reshape(1)

        new = None
        for i in range(n + 1):
            for number in reversed(range(layers)):
                block, g = grads[number][i]
                new = adamw(number, block, factor, g, weights, m, v, new)
        return tuple(new)

    return jax.shard_map(
        step,
        mesh=mesh,
        in_specs=(P(("rep", "dp"), None, None),) * 2 + (P(None, None, None),) * 9,
        out_specs=(P("rep", None, None),) * 9,
        check_vma=False,
    )
```

time: 1070 us -> 1080 us (level)
  waiting for transfers between devices: 653 us -> 231 us
  Pallas kernels: 0 us -> 176 us
  matrix products: 206 us -> 347 us
  local copies, waits for them, and re-layouts: 8.42 us -> 147 us
  other arithmetic: 180 us -> 60.6 us
  starting transfers between devices: 0.06 us -> 50.9 us
  blocking collectives: 0 us -> 46.6 us
    psum x1 -> x0, waiting for transfers between devices: 653 us -> none  [step(): summed[number] = [lax.psum(by_w[name], 'dp') for name in NAMES]]
    ppermute x0 -> x40, waiting for transfers between devices: none -> 231 us  [the longest x10 200 us: around(): lax.ppermute(block, 'dp', right)]
    pallas_call x0 -> x10, Pallas kernels: none -> 176 us  [adamw(): pl.pallas_call(adamw_kernel, grid_spec=pltpu.PrefetchScalarGridSpec(num_s...]
    dot_general x15 -> x18, matrix products: 206 us -> 347 us  [dot(): lax.dot_general(a, b, (((da,), (db,)), ((), ())), preferred_element_type=...]
    convert_element_type x2, other arithmetic: 141 us -> 16.5 us  [normed(): return (wide * scale).astype(BF16)]
    slice x0 -> x34, local copies, waits for them, and re-layouts: none -> 89.5 us  [the longest x2 21.8 us: step(): hidden = (jax.nn.silu(dot(a, w_gate[0])) * dot(a, w_up[0])).astype(BF16)]
    ppermute x0 -> x40, starting transfers between devices: none -> 50.9 us  [the longest x10 25.9 us: around(): lax.ppermute(after[half:], 'dp', left)]
    psum x0 -> x1, blocking collectives: none -> 46.6 us  [step(): total = lax.psum(squares, 'dp') + common]
  transfers between devices with their start and end apart: 1 -> 40, of which waited for: 1 -> 9; matrix products, arithmetic and copies ran while one was open for 0% -> 33% of each run, Pallas kernels for 0% -> 15%
where the time goes in v1:
time: 1080 us; the launch traced here: 1070 us
  matrix products  347 us (32%)
  waiting for transfers between devices  231 us (21%)
  Pallas kernels  176 us (16%)
  local copies, waits for them, and re-layouts  147 us (14%)
  other arithmetic  60.6 us (6%)
  starting transfers between devices  50.9 us (5%)
  blocking collectives  46.6 us (4%)
    dot_general x18, matrix products, dot(): lax.dot_general(a, b, (((da,), (db,)), ((), ())), preferred_element_type=...  347 us
    ppermute x10, waiting for transfers between devices, around(): lax.ppermute(block, 'dp', right)  200 us
    pallas_call x10, Pallas kernels, adamw(): pl.pallas_call(adamw_kernel, grid_spec=pltpu.PrefetchScalarGridSpec(num_s...  176 us
    psum x1, blocking collectives, step(): total = lax.psum(squares, 'dp') + common  46.6 us
    ppermute x10, waiting for transfers between devices, around(): lax.ppermute(before[:half], 'dp', right)  30.3 us
    ppermute x10, starting transfers between devices, around(): lax.ppermute(after[half:], 'dp', left)  25.9 us
    dynamic_update_slice x10, local copies, waits for them, and re-layouts, gathered(): every = lax.dynamic_update_slice(every, part[None], ((me + away) % n, 0, 0))  25.5 us
    slice x2, local copies, waits for them, and re-layouts, step(): hidden = (jax.nn.silu(dot(a, w_gate[0])) * dot(a, w_up[0])).astype(BF16)  21.8 us
  transfers between devices with their start and end apart: 40, of which 9 were waited for; matrix products, arithmetic and copies ran while one was open for 33% of the time, Pallas kernels for 15%

profile of v1, /device:TPU:112, one launch (start us, length us, event | category | flops | bytes accessed | tf_op | source)
XLA Modules:
  0.0 1069.5 jit_solution(5517355223550324008)
XLA Ops:
  20.8 22.7 %bitcast_dynamic-update-slice_fusion.9 = (bf16[4,1024,1024]{2,1,0:T(8,128)(2,1)}, bf16[1024,1024]{1,0:T(8,128)(2,1)}) fusion(bf16[4,1024,1024]{2,1,0:T(8,128)(2,1)} %broadcast.98.clone, s32[]{:T(128)S(6)} %select_n.89, bf16[2,3200,1024]{2,1,0:T(8,128)(2,1)} %refs_5_.19, f32[1024,3200]{1,0:T(8,128)} %fusion.87, bf16[1,1024,1024]{2,1,0:T(8,128)(2,1)S(1)} %copy-done.23, ...), kind=kOutput, calls=%fused_computation.115 | convolution fusion | flops 13449822208 | bytes 34607108 | tf_op jit(solution)/shard_map/dot_general | solution.py:22
  72.0 23.5 %fusion.84 = f32[1024,1024]{1,0:T(8,128)} fusion(bf16[1024,3200]{1,0:T(8,128)(2,1)} %convolution_convert_fusion.2, f32[1024,3200]{1,0:T(8,128)} %fusion.89, bf16[1024,1024]{1,0:T(8,128)(2,1)} %get-tuple-element.210, f32[1024]{0:T(1024)S(1)} %fusion.93, bf16[2,1024,3200]{2,1,0:T(8,128)(2,1)} %refs_3_.19, bf16[2,1024,3200]{2,1,0:T(8,128)(2,1)} %refs_4_.19), kind=kOutput, calls=%fused_computation.117 | convolution fusion | flops 13460963328 | bytes 39063552 | tf_op jit(solution)/shard_map/dot_general | solution.py:22
  186.9 30.0 %collective-permute-done = bf16[1024,1024]{1,0:T(8,128)(2,1)} collective-permute-done((bf16[1024,1024]{1,0:T(8,128)(2,1)}, bf16[1024,1024]{1,0:T(8,128)(2,1)}, u32[]{:S(2)}, u32[]{:S(2)}) %collective-permute-start) | collective-permute-done | bytes 2097184 | tf_op jit(solution)/shard_map/ppermute | solution.py:87
  243.6 18.2 %collective-permute-done.8 = bf16[1024,1024]{1,0:T(8,128)(2,1)} collective-permute-done((bf16[1024,1024]{1,0:T(8,128)(2,1)S(1)}, bf16[1024,1024]{1,0:T(8,128)(2,1)}, u32[]{:S(2)}, u32[]{:S(2)}) %collective-permute-start.8) | collective-permute-done | bytes 2097184 | tf_op jit(solution)/shard_map/ppermute | solution.py:87
  281.7 25.1 %collective-permute-done.4 = bf16[1024,1024]{1,0:T(8,128)(2,1)} collective-permute-done((bf16[1024,1024]{1,0:T(8,128)(2,1)}, bf16[1024,1024]{1,0:T(8,128)(2,1)}, u32[]{:S(2)}, u32[]{:S(2)}) %collective-permute-start.4) | collective-permute-done | bytes 2097184 | tf_op jit(solution)/shard_map/ppermute | solution.py:87
  321.4 30.3 %collective-permute-done.2 = bf16[512,1024]{1,0:T(8,128)(2,1)S(1)} collective-permute-done((bf16[512,1024]{1,0:T(8,128)(2,1)S(1)}, bf16[512,1024]{1,0:T(8,128)(2,1)S(1)}, u32[]{:S(2)}, u32[]{:S(2)}) %collective-permute-start.2) | collective-permute-done | bytes 1048608 | tf_op jit(solution)/shard_map/ppermute | solution.py:88
  368.6 18.7 %fusion.59 = f32[4096,1280]{1,0:T(8,128)} fusion(bf16[4096,1024]{1,0:T(8,128)(2,1)} %fusion.9, bf16[1024,640]{1,0:T(8,128)(2,1)} %slice.199, bf16[1024,640]{1,0:T(8,128)(2,1)} %get-tuple-element.217), kind=kOutput, calls=%fused_computation.69 | convolution fusion | flops 10742661120 | bytes 31981568 | tf_op jit(solution)/shard_map/dot_general | solution.py:22
  423.4 22.6 %fusion.47 = bf16[1280,1024]{1,0:T(8,128)(2,1)} fusion(bf16[4096,1024]{1,0:T(8,128)(2,1)} %bitcast.145, f32[4096,1280]{1,0:T(8,128)} %fusion.55, f32[4096,1280]{1,0:T(8,128)} %fusion.59), kind=kOutput, calls=%fused_computation.61 | convolution fusion | flops 10770186240 | bytes 52953088 | tf_op jit(solution)/shard_map/dot_general | solution.py:22
  446.0 25.1 %fusion.34 = bf16[1024,1280]{1,0:T(8,128)(2,1)} fusion(bf16[4096,1024]{1,0:T(8,128)(2,1)} %fusion.9, f32[4096,1280]{1,0:T(8,128)} %fusion.55, bf16[4096,1280]{1,0:T(8,128)(2,1)} %convolution_convert_fusion.1, f32[4096,1280]{1,0:T(8,128)} %fusion.59), kind=kOutput, calls=%fused_computation.56 | convolution fusion | flops 10796400640 | bytes 63438848 | tf_op jit(solution)/shard_map/dot_general | solution.py:22
  471.2 23.2 %fusion.40 = bf16[1024,1280]{1,0:T(8,128)(2,1)} fusion(bf16[4096,1024]{1,0:T(8,128)(2,1)} %fusion.9, bf16[4096,1280]{1,0:T(8,128)(2,1)} %convolution_convert_fusion.1, f32[4096,1280]{1,0:T(8,128)} %fusion.59), kind=kOutput, calls=%fused_computation.58 | convolution fusion | flops 10775429120 | bytes 42467328 | tf_op jit(solution)/shard_map/dot_general | solution.py:22
  510.9 18.7 %fusion.70 = f32[4096,1280]{1,0:T(8,128)} fusion(bf16[4096,1024]{1,0:T(8,128)(2,1)} %fusion.8, bf16[1024,640]{1,0:T(8,128)(2,1)S(1)} %copy-done.27, bf16[1024,640]{1,0:T(8,128)(2,1)S(1)} %copy-done.32), kind=kOutput, calls=%fused_computation.80 | convolution fusion | flops 10742661120 | bytes 31981568 | tf_op jit(solution)/shard_map/dot_general | solution.py:22
  565.1 22.6 %fusion.46 = bf16[1280,1024]{1,0:T(8,128)(2,1)} fusion(bf16[4096,1024]{1,0:T(8,128)(2,1)} %bitcast.31, f32[4096,1280]{1,0:T(8,128)} %fusion.66, f32[4096,1280]{1,0:T(8,128)} %fusion.70), kind=kOutput, calls=%fused_computation.60 | convolution fusion | flops 10770186240 | bytes 52953088 | tf_op jit(solution)/shard_map/dot_general | solution.py:22
  587.7 25.2 %fusion.37 = bf16[1024,1280]{1,0:T(8,128)(2,1)} fusion(bf16[4096,1024]{1,0:T(8,128)(2,1)} %fusion.8, f32[4096,1280]{1,0:T(8,128)} %fusion.66, bf16[4096,1280]{1,0:T(8,128)(2,1)} %convolution_convert_fusion, f32[4096,1280]{1,0:T(8,128)} %fusion.70), kind=kOutput, calls=%fused_computation.57 | convolution fusion | flops 10796400640 | bytes 63438848 | tf_op jit(solution)/shard_map/dot_general | solution.py:22
  618.6 23.3 %fusion.43 = bf16[1024,1280]{1,0:T(8,128)(2,1)} fusion(bf16[4096,1024]{1,0:T(8,128)(2,1)} %fusion.8, bf16[4096,1280]{1,0:T(8,128)(2,1)} %convolution_convert_fusion, f32[4096,1280]{1,0:T(8,128)} %fusion.70), kind=kOutput, calls=%fused_computation.59 | convolution fusion | flops 10775429120 | bytes 42467328 | tf_op jit(solution)/shard_map/dot_general | solution.py:22
  653.6 24.7 %collective-permute-done.32.refs_1_ = bf16[1024,640]{1,0:T(8,128)(2,1)} collective-permute-done((bf16[1024,640]{1,0:T(8,128)(2,1)}, bf16[1024,640]{1,0:T(8,128)(2,1)}, u32[]{:S(2)}, u32[]{:S(2)}) %collective-permute-start.32) | collective-permute-done | bytes 1310752 | tf_op jit(solution)/shard_map/ppermute | solution.py:87
  680.0 26.4 %collective-permute-done.28.refs_0_ = bf16[1024,640]{1,0:T(8,128)(2,1)S(1)} collective-permute-done((bf16[1024,640]{1,0:T(8,128)(2,1)}, bf16[1024,640]{1,0:T(8,128)(2,1)S(1)}, u32[]{:S(2)}, u32[]{:S(2)}) %collective-permute-start.28) | collective-permute-done | bytes 1310752 | tf_op jit(solution)/shard_map/ppermute | solution.py:87
  706.4 28.1 %collective-permute-done.24.refs_2_ = bf16[640,1024]{1,0:T(8,128)(2,1)S(1)} collective-permute-done((bf16[640,1024]{1,0:T(8,128)(2,1)}, bf16[640,1024]{1,0:T(8,128)(2,1)S(1)}, u32[]{:S(2)}, u32[]{:S(2)}) %collective-permute-start.24) | collective-permute-done | bytes 1310752 | tf_op jit(solution)/shard_map/ppermute | solution.py:87
  735.8 26.8 %collective-permute-done.20.refs_1_ = bf16[1024,640]{1,0:T(8,128)(2,1)S(1)} collective-permute-done((bf16[1024,640]{1,0:T(8,128)(2,1)S(1)}, bf16[1024,640]{1,0:T(8,128)(2,1)S(1)}, u32[]{:S(2)}, u32[]{:S(2)}) %collective-permute-start.20) | collective-permute-done | bytes 1310752 | tf_op jit(solution)/shard_map/ppermute | solution.py:87
  765.9 21.1 %collective-permute-done.16.refs_0_ = bf16[1024,640]{1,0:T(8,128)(2,1)} collective-permute-done((bf16[1024,640]{1,0:T(8,128)(2,1)}, bf16[1024,640]{1,0:T(8,128)(2,1)}, u32[]{:S(2)}, u32[]{:S(2)}) %collective-permute-start.16) | collective-permute-done | bytes 1310752 | tf_op jit(solution)/shard_map/ppermute | solution.py:87
  799.3 46.6 %psum.7 = f32[]{:T(128)} all-reduce(f32[]{:T(128)S(6)} %add.222), channel_id=1, replica_groups=mesh['rep'=4,'dp'=4] {'dp'}, use_global_device_ids=true, to_apply=%region_11.12 | all-reduce | flops 1 | bytes 8 | tf_op jit(solution)/shard_map/psum | solution.py:140
  875.5 18.1 %adamw.11 = (bf16[2,1024,3200]{2,1,0:T(8,128)(2,1)}, bf16[2,1024,3200]{2,1,0:T(8,128)(2,1)}, bf16[2,3200,1024]{2,1,0:T(8,128)(2,1)}, f32[2,1024,3200]{2,1,0:T(8,...) custom-call(s32[2]{0:T(128)S(1)} %get-tuple-element.213.at, ...), custom_call_target="tpu_custom_call", output_to_operand_aliasing={{0}: (14, {}), {1}: (15, {}), {2}: (16, {}), {3}: (17, {}),... | custom-call | flops 1769472000 | bytes 43253760 | tf_op jit(solution)/shard_map/adamw/pallas_call | solution.py:64
  942.4 17.8 %adamw.14 = (bf16[2,1024,3200]{2,1,0:T(8,128)(2,1)}, bf16[2,1024,3200]{2,1,0:T(8,128)(2,1)}, bf16[2,3200,1024]{2,1,0:T(8,128)(2,1)}, f32[2,1024,3200]{2,1,0:T(8,...) custom-call(s32[2]{0:T(128)S(1)} %pad_add_fusion.5.at, ...), custom_call_target="tpu_custom_call", output_to_operand_aliasing={{0}: (14, {}), {1}: (15, {}), {2}: (16, {}), {3}: (17, {}),... | custom-call | flops 1769472000 | bytes 43253760 | tf_op jit(solution)/shard_map/adamw/pallas_call | solution.py:64
  982.9 17.8 %adamw.16 = (bf16[2,1024,3200]{2,1,0:T(8,128)(2,1)}, bf16[2,1024,3200]{2,1,0:T(8,128)(2,1)}, bf16[2,3200,1024]{2,1,0:T(8,128)(2,1)}, f32[2,1024,3200]{2,1,0:T(8,...) custom-call(s32[2]{0:T(128)S(1)} %pad_add_fusion.6.at, ...), custom_call_target="tpu_custom_call", output_to_operand_aliasing={{0}: (14, {}), {1}: (15, {}), {2}: (16, {}), {3}: (17, {}),... | custom-call | flops 1769472000 | bytes 43253760 | tf_op jit(solution)/shard_map/adamw/pallas_call | solution.py:64
  1005.2 17.8 %adamw.17 = (bf16[2,1024,3200]{2,1,0:T(8,128)(2,1)}, bf16[2,1024,3200]{2,1,0:T(8,128)(2,1)}, bf16[2,3200,1024]{2,1,0:T(8,128)(2,1)}, f32[2,1024,3200]{2,1,0:T(8,...) custom-call(s32[2]{0:T(128)S(1)} %pad_add_fusion.2.at, ...), custom_call_target="tpu_custom_call", output_to_operand_aliasing={{0}: (14, {}), {1}: (15, {}), {2}: (16, {}), {3}: (17, {}),... | custom-call | flops 1769472000 | bytes 43253760 | tf_op jit(solution)/shard_map/adamw/pallas_call | solution.py:64
  (257 shorter events, 484.9 us)
Async XLA Ops:
  123.9 141.5 %collective-permute-start.13 = (bf16[1024,1024]{1,0:T(8,128)(2,1)}, bf16[1024,1024]{1,0:T(8,128)(2,1)}, u32[]{:S(2)}, u32[]{:S(2)}) collective-permute-start(bf16[1024,1024]{1,0:T(8,128)(2,1)} %get-tuple-element.184), channel_id=1, source_target_pairs={{0,3},{1,0},{2,1},{3,2},{4,7},{5,4},{6,5},{7,6},{8,11},{9,8},{10,9... | collective-permute-start | bytes 6291464 | tf_op jit(solution)/shard_map/ppermute | solution.py:87
  125.4 91.4 %collective-permute-start = (bf16[1024,1024]{1,0:T(8,128)(2,1)}, bf16[1024,1024]{1,0:T(8,128)(2,1)}, u32[]{:S(2)}, u32[]{:S(2)}) collective-permute-start(bf16[1024,1024]{1,0:T(8,128)(2,1)} %get-tuple-element.210), channel_id=1, source_target_pairs={{0,1},{1,2},{2,3},{3,0},{4,5},{5,6},{6,7},{7,4},{8,9},{9,10},{10,1... | collective-permute-start | bytes 6291464 | tf_op jit(solution)/shard_map/ppermute | solution.py:87
  125.9 91.4 %collective-permute-start.1 = (bf16[1024,1024]{1,0:T(8,128)(2,1)}, bf16[1024,1024]{1,0:T(8,128)(2,1)}, u32[]{:S(2)}, u32[]{:S(2)}) collective-permute-start(bf16[1024,1024]{1,0:T(8,128)(2,1)} %get-tuple-element.210), channel_id=1, source_target_pairs={{0,3},{1,0},{2,1},{3,2},{4,7},{5,4},{6,5},{7,6},{8,11},{9,8},{10,9... | collective-permute-start | bytes 6291464 | tf_op jit(solution)/shard_map/ppermute | solution.py:87
  128.7 133.1 %collective-permute-start.8 = (bf16[1024,1024]{1,0:T(8,128)(2,1)S(1)}, bf16[1024,1024]{1,0:T(8,128)(2,1)}, u32[]{:S(2)}, u32[]{:S(2)}) collective-permute-start(bf16[1024,1024]{1,0:T(8,128)(2,1)S(1)} %bitcast.146), channel_id=1, source_target_pairs={{0,1},{1,2},{2,3},{3,0},{4,5},{5,6},{6,7},{7,4},{8,9},{9,10},{10,1... | collective-permute-start | bytes 6291464 | tf_op jit(solution)/shard_map/ppermute | solution.py:87
  178.8 91.3 %collective-permute-start.9 = (bf16[1024,1024]{1,0:T(8,128)(2,1)S(1)}, bf16[1024,1024]{1,0:T(8,128)(2,1)}, u32[]{:S(2)}, u32[]{:S(2)}) collective-permute-start(bf16[1024,1024]{1,0:T(8,128)(2,1)S(1)} %bitcast.147), channel_id=1, source_target_pairs={{0,3},{1,0},{2,1},{3,2},{4,7},{5,4},{6,5},{7,6},{8,11},{9,8},{10,9... | collective-permute-start | bytes 6291464 | tf_op jit(solution)/shard_map/ppermute | solution.py:87
  216.9 89.9 %collective-permute-start.4 = (bf16[1024,1024]{1,0:T(8,128)(2,1)}, bf16[1024,1024]{1,0:T(8,128)(2,1)}, u32[]{:S(2)}, u32[]{:S(2)}) collective-permute-start(bf16[1024,1024]{1,0:T(8,128)(2,1)} %bitcast.11), channel_id=1, source_target_pairs={{0,1},{1,2},{2,3},{3,0},{4,5},{5,6},{6,7},{7,4},{8,9},{9,10},{10,1... | collective-permute-start | bytes 6291464 | tf_op jit(solution)/shard_map/ppermute | solution.py:87
  217.4 93.8 %collective-permute-start.5 = (bf16[1024,1024]{1,0:T(8,128)(2,1)}, bf16[1024,1024]{1,0:T(8,128)(2,1)}, u32[]{:S(2)}, u32[]{:S(2)}) collective-permute-start(bf16[1024,1024]{1,0:T(8,128)(2,1)} %bitcast.11), channel_id=1, source_target_pairs={{0,3},{1,0},{2,1},{3,2},{4,7},{5,4},{6,5},{7,6},{8,11},{9,8},{10,9... | collective-permute-start | bytes 6291464 | tf_op jit(solution)/shard_map/ppermute | solution.py:87
  261.8 282.6 %collective-permute-start.14 = (bf16[512,1024]{1,0:T(8,128)(2,1)}, bf16[512,1024]{1,0:T(8,128)(2,1)}, u32[]{:S(2)}, u32[]{:S(2)}) collective-permute-start(bf16[512,1024]{1,0:T(8,128)(2,1)} %slice.205), channel_id=1, source_target_pairs={{0,1},{1,2},{2,3},{3,0},{4,5},{5,6},{6,7},{7,4},{8,9},{9,10},{10,1... | collective-permute-start | bytes 3145736 | tf_op jit(solution)/shard_map/ppermute | solution.py:88
  265.4 86.3 %collective-permute-start.2 = (bf16[512,1024]{1,0:T(8,128)(2,1)S(1)}, bf16[512,1024]{1,0:T(8,128)(2,1)S(1)}, u32[]{:S(2)}, u32[]{:S(2)}) collective-permute-start(bf16[512,1024]{1,0:T(8,128)(2,1)S(1)} %slice.194), channel_id=1, source_target_pairs={{0,1},{1,2},{2,3},{3,0},{4,5},{5,6},{6,7},{7,4},{8,9},{9,10},{10,1... | collective-permute-start | bytes 3145736 | tf_op jit(solution)/shard_map/ppermute | solution.py:88
  306.7 237.6 %collective-permute-start.15 = (bf16[512,1024]{1,0:T(8,128)(2,1)}, bf16[512,1024]{1,0:T(8,128)(2,1)}, u32[]{:S(2)}, u32[]{:S(2)}) collective-permute-start(bf16[512,1024]{1,0:T(8,128)(2,1)} %slice.206), channel_id=1, source_target_pairs={{0,3},{1,0},{2,1},{3,2},{4,7},{5,4},{6,5},{7,6},{8,11},{9,8},{10,9... | collective-permute-start | bytes 3145736 | tf_op jit(solution)/shard_map/ppermute | solution.py:88
  311.1 183.2 %collective-permute-start.10 = (bf16[512,1024]{1,0:T(8,128)(2,1)}, bf16[512,1024]{1,0:T(8,128)(2,1)}, u32[]{:S(2)}, u32[]{:S(2)}) collective-permute-start(bf16[512,1024]{1,0:T(8,128)(2,1)} %slice.203), channel_id=1, source_target_pairs={{0,1},{1,2},{2,3},{3,0},{4,5},{5,6},{6,7},{7,4},{8,9},{9,10},{10,1... | collective-permute-start | bytes 3145736 | tf_op jit(solution)/shard_map/ppermute | solution.py:88
  401.9 92.5 %collective-permute-start.11 = (bf16[512,1024]{1,0:T(8,128)(2,1)}, bf16[512,1024]{1,0:T(8,128)(2,1)}, u32[]{:S(2)}, u32[]{:S(2)}) collective-permute-start(bf16[512,1024]{1,0:T(8,128)(2,1)} %slice.204), channel_id=1, source_target_pairs={{0,3},{1,0},{2,1},{3,2},{4,7},{5,4},{6,5},{7,6},{8,11},{9,8},{10,9... | collective-permute-start | bytes 3145736 | tf_op jit(solution)/shard_map/ppermute | solution.py:88
  645.9 88.6 %collective-permute-start.24 = (bf16[640,1024]{1,0:T(8,128)(2,1)}, bf16[640,1024]{1,0:T(8,128)(2,1)S(1)}, u32[]{:S(2)}, u32[]{:S(2)}) collective-permute-start(bf16[640,1024]{1,0:T(8,128)(2,1)} %get-tuple-element.204.refs_2_), channel_id=1, source_target_pairs={{0,1},{1,2},{2,3},{3,0},{4,5},{5,6},{6,7},{7,4},{8,9},{9,10},{10,1... | collective-permute-start | bytes 3932168 | tf_op jit(solution)/shard_map/ppermute | solution.py:87
  648.6 114.0 %collective-permute-start.20 = (bf16[1024,640]{1,0:T(8,128)(2,1)S(1)}, bf16[1024,640]{1,0:T(8,128)(2,1)S(1)}, u32[]{:S(2)}, u32[]{:S(2)}) collective-permute-start(bf16[1024,640]{1,0:T(8,128)(2,1)S(1)} %get-tuple-element.206.refs_1_), channel_id=1, source_target_pairs={{0,1},{1,2},{2,3},{3,0},{4,5},{5,6},{6,7},{7,4},{8,9},{9,10},{10,1... | collective-permute-start | bytes 3932168 | tf_op jit(solution)/shard_map/ppermute | solution.py:87
  651.6 135.4 %collective-permute-start.38 = (bf16[640,1024]{1,0:T(8,128)(2,1)}, bf16[640,1024]{1,0:T(8,128)(2,1)}, u32[]{:S(2)}, u32[]{:S(2)}) collective-permute-start(bf16[640,1024]{1,0:T(8,128)(2,1)} %get-tuple-element.198.refs_2_), channel_id=1, source_target_pairs={{0,3},{1,0},{2,1},{3,2},{4,7},{5,4},{6,5},{7,6},{8,11},{9,8},{10,9... | collective-permute-start | bytes 3932168 | tf_op jit(solution)/shard_map/ppermute | solution.py:87
  678.3 108.6 %collective-permute-start.16 = (bf16[1024,640]{1,0:T(8,128)(2,1)}, bf16[1024,640]{1,0:T(8,128)(2,1)}, u32[]{:S(2)}, u32[]{:S(2)}) collective-permute-start(bf16[1024,640]{1,0:T(8,128)(2,1)} %get-tuple-element.208.refs_0_), channel_id=1, source_target_pairs={{0,1},{1,2},{2,3},{3,0},{4,5},{5,6},{6,7},{7,4},{8,9},{9,10},{10,1... | collective-permute-start | bytes 3932168 | tf_op jit(solution)/shard_map/ppermute | solution.py:87
  706.4 148.0 %collective-permute-start.34 = (bf16[1024,640]{1,0:T(8,128)(2,1)}, bf16[1024,640]{1,0:T(8,128)(2,1)}, u32[]{:S(2)}, u32[]{:S(2)}) collective-permute-start(bf16[1024,640]{1,0:T(8,128)(2,1)} %get-tuple-element.200.refs_1_), channel_id=1, source_target_pairs={{0,3},{1,0},{2,1},{3,2},{4,7},{5,4},{6,5},{7,6},{8,11},{9,8},{10,9... | collective-permute-start | bytes 3932168 | tf_op jit(solution)/shard_map/ppermute | solution.py:87
  734.5 120.5 %collective-permute-start.30 = (bf16[1024,640]{1,0:T(8,128)(2,1)}, bf16[1024,640]{1,0:T(8,128)(2,1)}, u32[]{:S(2)}, u32[]{:S(2)}) collective-permute-start(bf16[1024,640]{1,0:T(8,128)(2,1)} %get-tuple-element.202.refs_0_), channel_id=1, source_target_pairs={{0,3},{1,0},{2,1},{3,2},{4,7},{5,4},{6,5},{7,6},{8,11},{9,8},{10,9... | collective-permute-start | bytes 3932168 | tf_op jit(solution)/shard_map/ppermute | solution.py:87
  762.6 133.0 %collective-permute-start.26 = (bf16[640,1024]{1,0:T(8,128)(2,1)}, bf16[640,1024]{1,0:T(8,128)(2,1)}, u32[]{:S(2)}, u32[]{:S(2)}) collective-permute-start(bf16[640,1024]{1,0:T(8,128)(2,1)} %get-tuple-element.204.refs_2_), channel_id=1, source_target_pairs={{0,3},{1,0},{2,1},{3,2},{4,7},{5,4},{6,5},{7,6},{8,11},{9,8},{10,9... | collective-permute-start | bytes 3932168 | tf_op jit(solution)/shard_map/ppermute | solution.py:87
  787.0 128.9 %collective-permute-start.22 = (bf16[1024,640]{1,0:T(8,128)(2,1)}, bf16[1024,640]{1,0:T(8,128)(2,1)}, u32[]{:S(2)}, u32[]{:S(2)}) collective-permute-start(bf16[1024,640]{1,0:T(8,128)(2,1)} %copy-done.4), channel_id=1, source_target_pairs={{0,3},{1,0},{2,1},{3,2},{4,7},{5,4},{6,5},{7,6},{8,11},{9,8},{10,9... | collective-permute-start | bytes 3932168 | tf_op jit(solution)/shard_map/ppermute | solution.py:87
  787.0 132.1 %collective-permute-start.18 = (bf16[1024,640]{1,0:T(8,128)(2,1)}, bf16[1024,640]{1,0:T(8,128)(2,1)}, u32[]{:S(2)}, u32[]{:S(2)}) collective-permute-start(bf16[1024,640]{1,0:T(8,128)(2,1)} %get-tuple-element.208.refs_0_), channel_id=1, source_target_pairs={{0,3},{1,0},{2,1},{3,2},{4,7},{5,4},{6,5},{7,6},{8,11},{9,8},{10,9... | collective-permute-start | bytes 3932168 | tf_op jit(solution)/shard_map/ppermute | solution.py:87
  855.0 87.5 %collective-permute-start.39 = (bf16[320,1024]{1,0:T(8,128)(2,1)}, bf16[320,1024]{1,0:T(8,128)(2,1)}, u32[]{:S(2)}, u32[]{:S(2)}) collective-permute-start(bf16[320,1024]{1,0:T(8,128)(2,1)} %slice.229), channel_id=1, source_target_pairs={{0,3},{1,0},{2,1},{3,2},{4,7},{5,4},{6,5},{7,6},{8,11},{9,8},{10,9... | collective-permute-start | bytes 1966088 | tf_op jit(solution)/shard_map/ppermute | solution.py:88
  915.9 86.0 %collective-permute-start.35 = (bf16[512,640]{1,0:T(8,128)(2,1)}, bf16[512,640]{1,0:T(8,128)(2,1)}, u32[]{:S(2)}, u32[]{:S(2)}) collective-permute-start(bf16[512,640]{1,0:T(8,128)(2,1)} %slice.227), channel_id=1, source_target_pairs={{0,3},{1,0},{2,1},{3,2},{4,7},{5,4},{6,5},{7,6},{8,11},{9,8},{10,9... | collective-permute-start | bytes 1966088 | tf_op jit(solution)/shard_map/ppermute | solution.py:88
  939.3 87.4 %collective-permute-start.31 = (bf16[512,640]{1,0:T(8,128)(2,1)}, bf16[512,640]{1,0:T(8,128)(2,1)}, u32[]{:S(2)}, u32[]{:S(2)}) collective-permute-start(bf16[512,640]{1,0:T(8,128)(2,1)} %slice.225), channel_id=1, source_target_pairs={{0,3},{1,0},{2,1},{3,2},{4,7},{5,4},{6,5},{7,6},{8,11},{9,8},{10,9... | collective-permute-start | bytes 1966088 | tf_op jit(solution)/shard_map/ppermute | solution.py:88
  (56 other events, 1680.7 us)

commit v2 on v1

v2 whole, which is shorter than its diff:
```python
import functools

import jax
import jax.numpy as jnp
from jax import lax
from jax.experimental import pallas as pl
from jax.experimental.pallas import tpu as pltpu
from jax.sharding import PartitionSpec as P

F32, BF16 = jnp.float32, jnp.bfloat16
ANY, VMEM = pl.ANY, pltpu.VMEM
LANES = 128
WIDE = 512
TILE = 256
ROWS = 512
FEW = 128
TURN = 256
OWN = (640, 384)


def dot(a, b, da=1, db=0):
    return lax.dot_general(a, b, (((da,), (db,)), ((), ())), preferred_element_type=F32)


def aligned(i, size):
    return pl.multiple_of(i * size, size)


def scale_of(wide):
    return lax.rsqrt(jnp.mean(wide**2, -1, keepdims=True) + 1e-6)


def gated(a, dout, w_gate, w_up, w_down):
    gate, up = dot(a, w_gate), dot(a, w_up)
    by_hidden = dot(dout, w_down, 1, 1).astype(BF16).astype(F32)
    s = jax.nn.sigmoid(gate)
    silu = gate * s
    hidden = (silu * up).astype(BF16)
    by_up = (by_hidden * silu).astype(BF16)
    by_gate = (by_hidden * up * (s * (1 + gate * (1 - s)))).astype(BF16)
    return hidden, by_gate, by_up


def gradients_kernel(
    n, count, x, dy, w_gate, w_up, w_down,
    first_gate, first_up, first_down, common_gate, common_up, common_down, last_gate, last_up, last_down, factor,
    x_all, dy_all, h_all, by_all, h_own, by_own,
    a_all, d_all, a_t, d_t, chain_gate, chain_up, chain_down, unit_gate, unit_up, unit_down, out_gate, out_up, out_down,
    hidden, by_gate, by_up, total, squares, square,
    chain_sem, unit_sem, out_sem, load_sem, send_sem, recv_sem, square_send, square_recv,
):
    tokens, d = x.shape
    ff = w_gate.shape[2]
    half = tokens // 2
    me = lax.axis_index("dp")
    right, left, far = lax.rem(me + 1, n), lax.rem(me + n - 1, n), lax.rem(me + 2, n)

    barrier = pltpu.get_barrier_semaphore()
    for other in (right, left, far):
        pl.semaphore_signal(barrier, inc=1, device_id={"dp": other}, device_id_type=pl.DeviceIdType.MESH)
    pl.semaphore_wait(barrier, n - 1)

    def send(src, dst, sems, to):
        return pltpu.make_async_remote_copy(
            src_ref=src, dst_ref=dst, send_sem=sems[0], recv_sem=sems[1], device_id={"dp": to}, device_id_type=pl.DeviceIdType.MESH
        )

    def ring(number, own, place):
        sems = [(send_sem.at[number + k], recv_sem.at[number + k]) for k in range(4)]
        return (
            (send(own, place(me), sems[0], right), send(own, place(me), sems[1], left)),
            (send(place(left, 0), place(left, 0), sems[2], right), send(place(right, 1), place(right, 1), sems[3], left)),
        )

    def block_of(every):
        return lambda i, k=None: every.at[i] if k is None else every.at[i, pl.ds(k * half, half)]

    def columns_of(full, own):
        def place(i, k=None):
            columns = pl.ds(pl.multiple_of(i * own, LANES), own)
            return full.at[:, columns] if k is None else full.at[pl.ds(k * (d // 2), d // 2), columns]

        return place

    def rows_of(full, own):
        def place(i, k=None):
            if k is None:
                return full.at[pl.ds(pl.multiple_of(i * own, LANES), own)]
            return full.at[pl.ds(pl.multiple_of(i * own + k * (own // 2), own // 2), own // 2)]

        return place

    def start(copies):
        for copy in copies:
            copy.start()

    def wait(copies):
        for copy in copies:
            copy.wait()

    def run(copies):
        start(copies)
        wait(copies)

    dy_ring = ring(0, dy, block_of(dy_all))
    x_ring = ring(4, x, block_of(x_all))
    h_ring = ring(8, h_own, block_of(h_all))
    by_ring = ring(12, by_own, block_of(by_all))
    places = columns_of(last_gate, OWN[1]), columns_of(last_up, OWN[1]), rows_of(last_down, OWN[1])
    last_rings = [ring(16 + 4 * i, place(me), place) for i, place in enumerate(places)]
    last_steps = [[copy for one in last_rings for copy in one[k]] for k in range(2)]

    start(dy_ring[0])

    own_x, own_dy, own_h, own_by = (pl.ds(i * tokens, tokens) for i in range(4))

    def chain(layer, body):
        tiles, rest = ff // WIDE, ff % WIDE

        def copies(i, slot, width):
            at = pl.multiple_of(i * WIDE, LANES)
            return [
                pltpu.make_async_copy(w_gate.at[layer, :, pl.ds(at, width)], chain_gate.at[slot, :, pl.ds(0, width)], chain_sem.at[slot, 0]),
                pltpu.make_async_copy(w_up.at[layer, :, pl.ds(at, width)], chain_up.at[slot, :, pl.ds(0, width)], chain_sem.at[slot, 1]),
                pltpu.make_async_copy(w_down.at[layer, pl.ds(at, width)], chain_down.at[slot, pl.ds(0, width)], chain_sem.at[slot, 2]),
            ]

        def rows_loop(slot, width):
            def some(r, _):
                body(pl.ds(pl.multiple_of(r * ROWS, ROWS), ROWS), slot, width)
                return 0

            lax.fori_loop(0, tokens // ROWS, some, 0)

        def tile(i, _):
            slot = lax.rem(i, 2)
            wait(copies(i, slot, WIDE))

            @pl.when(i + 1 < tiles)
            def _():
                start(copies(i + 1, lax.rem(i + 1, 2), WIDE))

            if rest:

                @pl.when(i + 1 == tiles)
                def _():
                    start(copies(tiles, tiles % 2, rest))

            rows_loop(slot, WIDE)
            return 0

        start(copies(0, 0, WIDE))
        total[...] = jnp.zeros_like(total)
        lax.fori_loop(0, tiles, tile, 0)
        if rest:
            wait(copies(tiles, tiles % 2, rest))
            rows_loop(tiles % 2, rest)

    def forward(rows, slot, width):
        a, units = a_all[rows], pl.ds(0, width)
        gate, up = dot(a, chain_gate[slot, :, units]), dot(a, chain_up[slot, :, units])
        total[rows] += dot((jax.nn.silu(gate) * up).astype(BF16), chain_down[slot, units])

    def backward(rows, slot, width):
        units = pl.ds(0, width)
        to_gate, to_up = chain_gate[slot, :, units], chain_up[slot, :, units]
        there = pl.ds(pl.multiple_of(tokens + rows.start, ROWS), ROWS)
        _, gate, up = gated(a_all[rows], d_all[there], to_gate, to_up, chain_down[slot, units])
        total[rows] += dot(gate, to_gate, 1, 1) + dot(up, to_up, 1, 1)

    def each(rows, body, length=tokens):
        def some(r, _):
            body(pl.multiple_of(r * rows, rows))
            return 0

        lax.fori_loop(0, length // rows, some, 0)

    def at(part, r, rows):
        return pl.ds(pl.multiple_of(part * tokens + r, rows), rows)

    run(
        [
            pltpu.make_async_copy(x, d_all.at[own_x], load_sem.at[0]),
            pltpu.make_async_copy(dy, d_all.at[own_dy], load_sem.at[1]),
        ]
    )

    def norm_x(r):
        wide = d_all[at(0, r, FEW)].astype(F32)
        a_all[at(0, r, FEW)] = (wide * scale_of(wide)).astype(BF16)

    each(FEW, norm_x)
    chain(0, forward)

    def add_layer(r):
        h = d_all[at(0, r, FEW)] + total[at(0, r, FEW)].astype(BF16)
        d_all[at(2, r, FEW)] = h
        wide = h.astype(F32)
        a_all[at(0, r, FEW)] = (wide * scale_of(wide)).astype(BF16)

    each(FEW, add_layer)
    run([pltpu.make_async_copy(d_all.at[own_h], h_own, load_sem.at[0])])
    start(h_ring[0])
    chain(1, backward)

    def norm_back(r):
        wide = d_all[at(2, r, FEW)].astype(F32)
        scale = scale_of(wide)
        by_a = total[at(0, r, FEW)].astype(BF16).astype(F32)
        by_mean = jnp.sum(by_a * wide, -1, keepdims=True) * -0.5 * (scale * scale * scale)
        by_wide = by_a * scale + wide * (by_mean * (2.0 / d))
        d_all[at(3, r, FEW)] = d_all[at(1, r, FEW)] + by_wide.astype(BF16)

    each(FEW, norm_back)
    run([pltpu.make_async_copy(d_all.at[own_by], by_own, load_sem.at[0])])

    def load(states, own_states, outs, own_outs):
        copies = []
        for which, (every, own, there) in enumerate(((states, own_states, a_all), (outs, own_outs, d_all))):
            for away in range(n):
                i = lax.rem(me + away, n)
                rows = there.at[pl.ds(pl.multiple_of(i * tokens, tokens), tokens)]
                copies.append(pltpu.make_async_copy(own if away == 0 else every.at[i], rows, load_sem.at[which * n + away]))
        run(copies)

        def turn(r):
            rows = pl.ds(r, TURN)
            wide = a_all[rows].astype(F32)
            a = (wide * scale_of(wide)).astype(BF16)
            a_all[rows] = a
            a_t[:, rows] = a.T
            d_t[:, rows] = d_all[rows].T

        each(TURN, turn, n * tokens)

    squares[...] = jnp.zeros_like(squares)

    def gradients(layer, targets, between):
        mine = OWN[layer] // LANES
        lots = ff // LANES - (n - 1) * mine
        per = TILE // LANES
        tiles = lots // per

        def units(g):
            return pl.ds(pl.multiple_of(jnp.where(g < mine, me * mine + g, (n - 1) * mine + g) * LANES, LANES), LANES)

        def weight_copies(i, slot):
            copies = []
            for p in range(per):
                there, part = units(i * per + p), pl.ds(p * LANES, LANES)
                copies += [
                    pltpu.make_async_copy(w_gate.at[layer, :, there], unit_gate.at[slot, :, part], unit_sem.at[slot, 3 * p]),
                    pltpu.make_async_copy(w_up.at[layer, :, there], unit_up.at[slot, :, part], unit_sem.at[slot, 3 * p + 1]),
                    pltpu.make_async_copy(w_down.at[layer, there], unit_down.at[slot, part], unit_sem.at[slot, 3 * p + 2]),
                ]
            return copies

        def put(i, slot, act):
            for p in range(per):
                part = pl.ds(p * LANES, LANES)
                for condition, (to_gate, to_up, to_down) in targets(i * per + p, units(i * per + p)):
                    copies = [
                        pltpu.make_async_copy(out_gate.at[slot, :, part], to_gate, out_sem.at[slot, 3 * p]),
                        pltpu.make_async_copy(out_up.at[slot, :, part], to_up, out_sem.at[slot, 3 * p + 1]),
                        pltpu.make_async_copy(out_down.at[slot, part], to_down, out_sem.at[slot, 3 * p + 2]),
                    ]
                    if condition is None:
                        act(copies)
                    else:
                        pl.when(condition)(functools.partial(act, copies))

        def tile(i, _):
            slot = lax.rem(i, 2)
            wait(weight_copies(i, slot))

            @pl.when(i + 1 < tiles)
            def _():
                start(weight_copies(i + 1, lax.rem(i + 1, 2)))

            between(i)

            def some(r, _):
                rows = pl.ds(pl.multiple_of(r * ROWS, ROWS), ROWS)
                made = gated(a_all[rows], d_all[rows], unit_gate[slot], unit_up[slot], unit_down[slot])
                hidden[rows], by_gate[rows], by_up[rows] = made
                return 0

            lax.fori_loop(0, n * tokens // ROWS, some, 0)

            @pl.when(i >= 2)
            def _():
                put(i - 2, slot, wait)

            both = jnp.zeros((8, TILE), F32)
            for turned, by, out in ((a_t, by_gate, out_gate), (a_t, by_up, out_up), (d_t, hidden, out_down)):
                g = dot(turned[...], by[...]).astype(BF16)
                out[slot] = g.T if out is out_down else g
                wide = g.astype(F32)
                both += jnp.sum((wide * wide).reshape(d // 8, 8, TILE), 0)
            for p in range(per):
                part, is_mine = both[:, p * LANES : (p + 1) * LANES], i * per + p < mine
                squares[0] += jnp.where(is_mine, part, 0.0)
                squares[1] += jnp.where(is_mine, 0.0, part)
            put(i, slot, start)
            return 0

        start(weight_copies(0, 0))
        lax.fori_loop(0, tiles, tile, 0)
        for i in range(max(tiles - 2, 0), tiles):
            put(i, i % 2, wait)

    wait(dy_ring[0])
    start(dy_ring[1])
    wait(h_ring[0])
    start(h_ring[1])
    start(by_ring[0])
    start(x_ring[0])
    wait(dy_ring[1])
    wait(h_ring[1])
    load(h_all, h_own, dy_all, dy)

    def forward_on(i):
        @pl.when(i == 3)
        def _():
            wait(by_ring[0])
            start(by_ring[1])

        @pl.when(i == 6)
        def _():
            wait(x_ring[0])
            start(x_ring[1])

    gradients(1, lambda g, units: [(None, (last_gate.at[:, units], last_up.at[:, units], last_down.at[units]))], forward_on)
    start(last_steps[0])
    wait(by_ring[1])
    wait(x_ring[1])
    load(x_all, x, by_all, by_own)

    def first_targets(g, units):
        mine = OWN[0] // LANES
        own = pl.ds(pl.multiple_of(jnp.minimum(g, mine - 1) * LANES, LANES), LANES)
        rest = pl.ds(pl.multiple_of(jnp.maximum(g - mine, 0) * LANES, LANES), LANES)
        return [
            (g < mine, (first_gate.at[:, own], first_up.at[:, own], first_down.at[own])),
            (g >= mine, (common_gate.at[:, rest], common_up.at[:, rest], common_down.at[rest])),
        ]

    def last_on(i):
        @pl.when(i == 3)
        def _():
            wait(last_steps[0])
            start(last_steps[1])

    gradients(0, first_targets, last_on)

    square[me] = squares[0]
    swaps = [send(square.at[me], square.at[me], (square_send.at[k], square_recv.at[k]), to) for k, to in enumerate((right, left, far))]
    start(swaps)
    wait(swaps)
    wait(last_steps[1])
    every = squares[1]
    for i in range(n):
        every = every + square[i]
    every = jnp.sum(jnp.sum(every, 0, keepdims=True), 1, keepdims=True)
    factor[...] = jnp.broadcast_to(jnp.minimum(1.0, 0.5 * lax.rsqrt(every / count + 1e-30)), factor.shape)


def make_gradients(n, x, dy, w_gate, w_up, w_down):
    tokens, d = x.shape
    layers, _, ff = w_gate.shape
    assert n == 4 and layers == 2
    own, rest = OWN[0], ff - n * OWN[0]
    shape = jax.ShapeDtypeStruct
    every = shape((n, tokens, d), BF16)
    outs = [shape((d, own), BF16)] * 2 + [shape((own, d), BF16)] + [shape((d, rest), BF16)] * 2 + [shape((rest, d), BF16)]
    outs += [shape((d, ff), BF16)] * 2 + [shape((ff, d), BF16)] + [shape((8, LANES), F32)] + [every] * 4 + [shape((tokens, d), BF16)] * 2
    dma = pltpu.SemaphoreType.DMA
    scratch = [VMEM((n * tokens, d), BF16)] * 2 + [VMEM((d, n * tokens), BF16)] * 2
    scratch += [VMEM((2, d, WIDE), BF16)] * 2 + [VMEM((2, WIDE, d), BF16)]
    scratch += ([VMEM((2, d, TILE), BF16)] * 2 + [VMEM((2, TILE, d), BF16)]) * 2
    scratch += [VMEM((n * tokens, TILE), BF16)] * 3 + [VMEM((tokens, d), F32), VMEM((2, 8, LANES), F32), VMEM((n, 8, LANES), F32)]
    scratch += [dma((2, 3)), dma((2, 6)), dma((2, 6)), dma((2 * n,)), dma((28,)), dma((28,)), dma((3,)), dma((3,))]
    return pl.pallas_call(
        functools.partial(gradients_kernel, n, layers * 3 * d * ff),
        out_shape=outs,
        in_specs=[pl.BlockSpec(memory_space=ANY)] * 5,
        out_specs=[pl.BlockSpec(memory_space=ANY)] * 9 + [pl.BlockSpec(memory_space=VMEM)] + [pl.BlockSpec(memory_space=ANY)] * 6,
        scratch_shapes=scratch,
        compiler_params=pltpu.CompilerParams(collective_id=0, has_side_effects=True, vmem_limit_bytes=67043328),
        cost_estimate=pl.CostEstimate(flops=tokens * d * ff * 2 * 40, bytes_accessed=2**27, transcendentals=0),
        name="gradients",
    )(x, dy, w_gate, w_up, w_down)[:10]


def adamw_kernel(*refs):
    factor, grads, w, m, v = (refs[1], *(refs[i : i + 3] for i in (2, 5, 8, 11)))
    w_out, m_out, v_out = (refs[len(refs) - 9 + i : len(refs) - 6 + i] for i in (0, 3, 6))
    c = factor[0:1, 0:1]
    for i in range(3):
        g = grads[i][...].astype(F32) * c
        mm = 0.9 * m[i][0] + 0.1 * g
        vv = 0.95 * v[i][0] + 0.05 * g * g
        wide = w[i][0].astype(F32)
        step = mm * lax.rsqrt(vv + 1e-8) + 0.1 * wide
        w_out[i][0] = (wide - 0.02 * step).astype(BF16)
        m_out[i][0] = mm
        v_out[i][0] = vv


def adamw(layer, block, steps, factor, grads, weights, m, v, so_far):
    d, width = grads[0].shape
    at = jnp.asarray(block, jnp.int32).reshape(1)
    rows, down_rows = d // steps, width // steps
    by_column = pl.BlockSpec((rows, width), lambda i, at: (i, 0))
    by_row = pl.BlockSpec((down_rows, d), lambda i, at: (i, 0))
    column = pl.BlockSpec((1, rows, width), lambda i, at: (layer, i, at[0]))
    row = pl.BlockSpec((1, down_rows, d), lambda i, at: (layer, at[0] * steps + i, 0))
    whole = [column, column, row]
    shapes = [jax.ShapeDtypeStruct(a.shape, t) for t in (BF16, F32, F32) for a in weights]
    olds = () if so_far is None else tuple(so_far)
    elements = 3 * d * width
    return pl.pallas_call(
        adamw_kernel,
        grid_spec=pltpu.PrefetchScalarGridSpec(
            num_scalar_prefetch=1,
            grid=(steps,),
            in_specs=[pl.BlockSpec((8, LANES), lambda i, at: (0, 0)), by_column, by_column, by_row]
            + whole * 3
            + [pl.BlockSpec(memory_space=ANY)] * len(olds),
            out_specs=whole * 3,
        ),
        out_shape=shapes,
        input_output_aliases={14 + i: i for i in range(len(olds))},
        compiler_params=pltpu.CompilerParams(dimension_semantics=("arbitrary",), vmem_limit_bytes=56 * 2**20),
        cost_estimate=pl.CostEstimate(flops=elements * 900, bytes_accessed=elements * 22, transcendentals=elements),
        name="adamw",
    )(at, factor, *grads, *weights, *m, *v, *olds)


def solution(mesh):
    n = mesh.shape["dp"]
    to_right = [(i, (i + 1) % n) for i in range(n)]
    to_left = [(i, (i - 1) % n) for i in range(n)]

    def step(x, dy, *arrays):
        weights, m, v = (arrays[i : i + 3] for i in (0, 3, 6))
        me = lax.axis_index("dp")
        *gradients, factor = make_gradients(n, x[0], dy[0], *weights)
        mine, common, last = (gradients[i : i + 3] for i in (0, 3, 6))
        before = [lax.ppermute(g, "dp", to_right) for g in mine]
        after = [lax.ppermute(g, "dp", to_left) for g in mine]

        def update(layer, block, steps, g, new):
            return adamw(layer, block, steps, factor, g, weights, m, v, new)

        new = update(1, 0, 16, last, None)
        new = update(0, me, 8, mine, new)
        new = update(0, n, 8, common, new)
        top = [lax.ppermute(g[: g.shape[0] // 2], "dp", to_right) for g in before]
        bottom = [lax.ppermute(g[g.shape[0] // 2 :], "dp", to_left) for g in after]
        new = update(0, (me + n - 1) % n, 8, before, new)
        new = update(0, (me + 1) % n, 8, after, new)
        far = [jnp.concatenate(both) for both in zip(top, bottom, strict=True)]
        new = update(0, (me + 2) % n, 8, far, new)
        return tuple(new)

    return jax.shard_map(
        step,
        mesh=mesh,
        in_specs=(P(("rep", "dp"), None, None),) * 2 + (P(None, None, None),) * 9,
        out_specs=(P("rep", None, None),) * 9,
        check_vma=False,
    )
```

time: 1080 us -> 594 us (0.55)
  Pallas kernels: 176 us -> 532 us
  matrix products: 347 us -> 0 us
  waiting for transfers between devices: 231 us -> 26.4 us
  local copies, waits for them, and re-layouts: 147 us -> 9.96 us
  other arithmetic: 60.6 us -> 7.4 us
  blocking collectives: 46.6 us -> 0 us
  starting transfers between devices: 50.9 us -> 16.5 us
    pallas_call x0 -> x1, Pallas kernels: none -> 372 us  [make_gradients(): pl.pallas_call(functools.partial(gradients_kernel, n, layers * 3 * d * ff...]
    dot_general x18 -> x0, matrix products: 347 us -> none  [dot(): lax.dot_general(a, b, (((da,), (db,)), ((), ())), preferred_element_type=...]
    ppermute x40 -> x12, waiting for transfers between devices: 231 us -> 26.4 us  [the longest x3 26.4 us: step(): after = [lax.ppermute(g, 'dp', to_left) for g in mine]]
    slice x34 -> x6, local copies, waits for them, and re-layouts: 89.5 us -> 9.96 us  [the longest x3 6.01 us: step(): top = [lax.ppermute(g[:g.shape[0] // 2], 'dp', to_right) for g in before]]
    psum x1 -> x0, blocking collectives: 46.6 us -> none  [step(): total = lax.psum(squares, 'dp') + common]
    ppermute x40 -> x12, starting transfers between devices: 50.9 us -> 16.5 us  [the longest x3 6.65 us: step(): after = [lax.ppermute(g, 'dp', to_left) for g in mine]]
    dynamic_update_slice x10 -> x0, local copies, waits for them, and re-layouts: 25.5 us -> none  [gathered(): every = lax.dynamic_update_slice(every, part[None], ((me + away) % n, 0, 0))]
    reduce_sum x10 -> x0, other arithmetic: 23.8 us -> none  [the longest x6 12.9 us: step(): common += sum((jnp.sum(g.astype(F32) ** 2) for g in shared))]
  transfers between devices with their start and end apart: 40 -> 12, of which waited for: 9 -> 1; matrix products, arithmetic and copies ran while one was open for 33% -> 3% of each run, Pallas kernels for 15% -> 24%
where the time goes in v2:
time: 594 us; the launch traced here: 593 us
  Pallas kernels  532 us (90%)
  waiting for transfers between devices  26.4 us (4%)
  starting transfers between devices  16.5 us (3%)
  local copies, waits for them, and re-layouts  9.96 us (2%)
  other arithmetic  7.4 us (1%)
    pallas_call x1, Pallas kernels, make_gradients(): pl.pallas_call(functools.partial(gradients_kernel, n, layers * 3 * d * ff...  372 us
    pallas_call x6, Pallas kernels, adamw(): pl.pallas_call(adamw_kernel, grid_spec=pltpu.PrefetchScalarGridSpec(num_s...  159 us
    ppermute x3, waiting for transfers between devices, step(): after = [lax.ppermute(g, 'dp', to_left) for g in mine]  26.4 us
  transfers between devices with their start and end apart: 12, of which 1 were waited for; matrix products, arithmetic and copies ran while one was open for 3% of the time, Pallas kernels for 24%

profile of v2, /device:TPU:112, one launch (start us, length us, event | category | flops | bytes accessed | tf_op | source)
XLA Modules:
  0.0 592.8 jit_solution(4744114100800084538)
XLA Ops:
  0.6 372.3 %gradients.1 = (bf16[1024,640]{1,0:T(8,128)(2,1)}, bf16[1024,640]{1,0:T(8,128)(2,1)}, bf16[640,1024]{1,0:T(8,128)(2,1)}, bf16[1024,640]{1,0:T(8,128)(2,1)}, bf16...) custom-call(bf16[1024,1024]{1,0:T(8,128)(2,1)} %bitcast.6, ...), custom_call_target="tpu_custom_call" | custom-call | flops 268435456000 | bytes 134217728 | tf_op jit(solution)/shard_map/gradients/pallas_call | solution.py:383
  372.9 1.6 collective-permute-start.10
  375.0 0.9 collective-permute-start.4
  375.9 2.3 collective-permute-start.6
  378.3 26.4 %collective-permute-done.10.refs_4_ = bf16[640,1024]{1,0:T(8,128)(2,1)S(1)} collective-permute-done((bf16[640,1024]{1,0:T(8,128)(2,1)}, bf16[640,1024]{1,0:T(8,128)(2,1)S(1)}, u32[]{:S(2)}, u32[]{:S(2)}) %collective-permute-start.10) | collective-permute-done | bytes 1310752 | tf_op jit(solution)/shard_map/ppermute | solution.py:451
  404.7 2.7 collective-permute-start.2
  407.4 0.9 slice.29
  408.3 71.2 %adamw.6 = (bf16[2,1024,3200]{2,1,0:T(8,128)(2,1)}, bf16[2,1024,3200]{2,1,0:T(8,128)(2,1)}, bf16[2,3200,1024]{2,1,0:T(8,128)(2,1)}, f32[2,1024,3200]{2,1,0:T(8,1...) custom-call(s32[1]{0:T(128)} %constant.34.clone.1.refs_0_, ...), custom_call_target="tpu_custom_call" | custom-call | flops 8847360000 | bytes 216268800 | tf_op jit(solution)/shard_map/adamw/pallas_call | solution.py:422
  479.5 2.0 slice.28
  481.5 2.0 collective-permute-start.9
  483.5 2.0 slice.26
  485.5 1.1 slice.27
  486.6 3.2 collective-permute-start.7
  489.7 17.6 %adamw.7 = (bf16[2,1024,3200]{2,1,0:T(8,128)(2,1)}, bf16[2,1024,3200]{2,1,0:T(8,128)(2,1)}, bf16[2,3200,1024]{2,1,0:T(8,128)(2,1)}, f32[2,1024,3200]{2,1,0:T(8,1...) custom-call(s32[1]{0:T(128)} %bitcast.5.refs_0_, ...), custom_call_target="tpu_custom_call", output_to_operand_aliasing={{0}: (14, {}), {1}: (15, {}), {2}: (16, {}), {3}: (17, {}),... | custom-call | flops 1769472000 | bytes 43253760 | tf_op jit(solution)/shard_map/adamw/pallas_call | solution.py:422
  507.3 2.1 slice.24
  509.4 2.0 slice.25
  511.4 3.2 collective-permute-start.3
  514.6 17.6 %adamw.8 = (bf16[2,1024,3200]{2,1,0:T(8,128)(2,1)}, bf16[2,1024,3200]{2,1,0:T(8,128)(2,1)}, bf16[2,3200,1024]{2,1,0:T(8,128)(2,1)}, f32[2,1024,3200]{2,1,0:T(8,1...) custom-call(s32[1]{0:T(128)} %constant.33.clone.1.refs_0_, ...), custom_call_target="tpu_custom_call", output_to_operand_aliasing={{0}: (14, {}), {1}: (15, {}), {2}: (16, {}), {3}: (17, {}),... | custom-call | flops 1769472000 | bytes 43253760 | tf_op jit(solution)/shard_map/adamw/pallas_call | solution.py:422
  532.2 17.7 %adamw.9 = (bf16[2,1024,3200]{2,1,0:T(8,128)(2,1)}, bf16[2,1024,3200]{2,1,0:T(8,128)(2,1)}, bf16[2,3200,1024]{2,1,0:T(8,128)(2,1)}, f32[2,1024,3200]{2,1,0:T(8,1...) custom-call(s32[1]{0:T(128)} %bitcast.4.refs_0_, ...), custom_call_target="tpu_custom_call", output_to_operand_aliasing={{0}: (14, {}), {1}: (15, {}), {2}: (16, {}), {3}: (17, {}),... | custom-call | flops 1769472000 | bytes 43253760 | tf_op jit(solution)/shard_map/adamw/pallas_call | solution.py:422
  549.9 17.7 %adamw.10 = (bf16[2,1024,3200]{2,1,0:T(8,128)(2,1)}, bf16[2,1024,3200]{2,1,0:T(8,128)(2,1)}, bf16[2,3200,1024]{2,1,0:T(8,128)(2,1)}, f32[2,1024,3200]{2,1,0:T(8,...) custom-call(s32[1]{0:T(128)} %bitcast.3.refs_0_, ...), custom_call_target="tpu_custom_call", output_to_operand_aliasing={{0}: (14, {}), {1}: (15, {}), {2}: (16, {}), {3}: (17, {}),... | custom-call | flops 1769472000 | bytes 43253760 | tf_op jit(solution)/shard_map/adamw/pallas_call | solution.py:422
  567.6 2.5 pad_maximum_fusion.2.refs_4_
  570.0 2.5 pad_maximum_fusion.1.refs_3_
  572.5 2.5 pad_maximum_fusion.refs_2_
  575.0 17.6 %adamw.11 = (bf16[2,1024,3200]{2,1,0:T(8,128)(2,1)}, bf16[2,1024,3200]{2,1,0:T(8,128)(2,1)}, bf16[2,3200,1024]{2,1,0:T(8,128)(2,1)}, f32[2,1024,3200]{2,1,0:T(8,...) custom-call(s32[1]{0:T(128)} %bitcast.refs_0_, ...), custom_call_target="tpu_custom_call", output_to_operand_aliasing={{0}: (14, {}), {1}: (15, {}), {2}: (16, {}), {3}: (17, {}),... | custom-call | flops 1769472000 | bytes 43253760 | tf_op jit(solution)/shard_map/adamw/pallas_call | solution.py:422
  (20 shorter events, 0.6 us)
Async XLA Ops:
  372.9 31.7 %collective-permute-start.10 = (bf16[640,1024]{1,0:T(8,128)(2,1)}, bf16[640,1024]{1,0:T(8,128)(2,1)S(1)}, u32[]{:S(2)}, u32[]{:S(2)}) collective-permute-start(bf16[640,1024]{1,0:T(8,128)(2,1)} %get-tuple-element.67.refs_4_), channel_id=1, source_target_pairs={{0,3},{1,0},{2,1},{3,2},{4,7},{5,4},{6,5},{7,6},{8,11},{9,8},{10,9... | collective-permute-start | bytes 3932168 | tf_op jit(solution)/shard_map/ppermute | solution.py:451
  374.5 33.8 %collective-permute-start.8 = (bf16[640,1024]{1,0:T(8,128)(2,1)}, bf16[640,1024]{1,0:T(8,128)(2,1)}, u32[]{:S(2)}, u32[]{:S(2)}) collective-permute-start(bf16[640,1024]{1,0:T(8,128)(2,1)} %get-tuple-element.67.refs_4_), channel_id=1, source_target_pairs={{0,1},{1,2},{2,3},{3,0},{4,5},{5,6},{6,7},{7,4},{8,9},{9,10},{10,1... | collective-permute-start | bytes 3932168 | tf_op jit(solution)/shard_map/ppermute | solution.py:450
  375.0 106.5 %collective-permute-start.4 = (bf16[1024,640]{1,0:T(8,128)(2,1)}, bf16[1024,640]{1,0:T(8,128)(2,1)}, u32[]{:S(2)}, u32[]{:S(2)}) collective-permute-start(bf16[1024,640]{1,0:T(8,128)(2,1)} %get-tuple-element.66.refs_3_), channel_id=1, source_target_pairs={{0,1},{1,2},{2,3},{3,0},{4,5},{5,6},{6,7},{7,4},{8,9},{9,10},{10,1... | collective-permute-start | bytes 3932168 | tf_op jit(solution)/shard_map/ppermute | solution.py:450
  375.9 109.6 %collective-permute-start.6 = (bf16[1024,640]{1,0:T(8,128)(2,1)}, bf16[1024,640]{1,0:T(8,128)(2,1)S(1)}, u32[]{:S(2)}, u32[]{:S(2)}) collective-permute-start(bf16[1024,640]{1,0:T(8,128)(2,1)} %get-tuple-element.66.refs_3_), channel_id=1, source_target_pairs={{0,3},{1,0},{2,1},{3,2},{4,7},{5,4},{6,5},{7,6},{8,11},{9,8},{10,9... | collective-permute-start | bytes 3932168 | tf_op jit(solution)/shard_map/ppermute | solution.py:451
  378.3 108.3 %collective-permute-start = (bf16[1024,640]{1,0:T(8,128)(2,1)}, bf16[1024,640]{1,0:T(8,128)(2,1)}, u32[]{:S(2)}, u32[]{:S(2)}) collective-permute-start(bf16[1024,640]{1,0:T(8,128)(2,1)} %get-tuple-element.65.refs_2_), channel_id=1, source_target_pairs={{0,1},{1,2},{2,3},{3,0},{4,5},{5,6},{6,7},{7,4},{8,9},{9,10},{10,1... | collective-permute-start | bytes 3932168 | tf_op jit(solution)/shard_map/ppermute | solution.py:450
  404.7 74.9 %copy-start = (bf16[640,1024]{1,0:T(8,128)(2,1)}, bf16[640,1024]{1,0:T(8,128)(2,1)S(1)}, u32[]{:S(2)}) copy-start(bf16[640,1024]{1,0:T(8,128)(2,1)S(1)} %collective-permute-done.10.refs_4_) | copy-start | bytes 3932164
  404.7 104.7 %collective-permute-start.2 = (bf16[1024,640]{1,0:T(8,128)(2,1)}, bf16[1024,640]{1,0:T(8,128)(2,1)}, u32[]{:S(2)}, u32[]{:S(2)}) collective-permute-start(bf16[1024,640]{1,0:T(8,128)(2,1)} %get-tuple-element.65.refs_2_), channel_id=1, source_target_pairs={{0,3},{1,0},{2,1},{3,2},{4,7},{5,4},{6,5},{7,6},{8,11},{9,8},{10,9... | collective-permute-start | bytes 3932168 | tf_op jit(solution)/shard_map/ppermute | solution.py:451
  408.3 103.1 %collective-permute-start.11 = (bf16[320,1024]{1,0:T(8,128)(2,1)}, bf16[320,1024]{1,0:T(8,128)(2,1)}, u32[]{:S(2)}, u32[]{:S(2)}) collective-permute-start(bf16[320,1024]{1,0:T(8,128)(2,1)} %slice.29), channel_id=1, source_target_pairs={{0,3},{1,0},{2,1},{3,2},{4,7},{5,4},{6,5},{7,6},{8,11},{9,8},{10,9... | collective-permute-start | bytes 1966088 | tf_op jit(solution)/shard_map/ppermute | solution.py:460
  481.5 86.0 %collective-permute-start.9 = (bf16[320,1024]{1,0:T(8,128)(2,1)}, bf16[320,1024]{1,0:T(8,128)(2,1)}, u32[]{:S(2)}, u32[]{:S(2)}) collective-permute-start(bf16[320,1024]{1,0:T(8,128)(2,1)} %slice.28), channel_id=1, source_target_pairs={{0,1},{1,2},{2,3},{3,0},{4,5},{5,6},{6,7},{7,4},{8,9},{9,10},{10,1... | collective-permute-start | bytes 1966088 | tf_op jit(solution)/shard_map/ppermute | solution.py:459
  485.5 21.8 %copy-start.1 = (bf16[1024,640]{1,0:T(8,128)(2,1)}, bf16[1024,640]{1,0:T(8,128)(2,1)S(1)}, u32[]{:S(2)}) copy-start(bf16[1024,640]{1,0:T(8,128)(2,1)S(1)} %collective-permute-done.6.refs_3_) | copy-start | bytes 3932164
  485.5 84.6 %collective-permute-start.5 = (bf16[512,640]{1,0:T(8,128)(2,1)}, bf16[512,640]{1,0:T(8,128)(2,1)}, u32[]{:S(2)}, u32[]{:S(2)}) collective-permute-start(bf16[512,640]{1,0:T(8,128)(2,1)} %slice.26), channel_id=1, source_target_pairs={{0,1},{1,2},{2,3},{3,0},{4,5},{5,6},{6,7},{7,4},{8,9},{9,10},{10,1... | collective-permute-start | bytes 1966088 | tf_op jit(solution)/shard_map/ppermute | solution.py:459
  486.6 83.5 %collective-permute-start.7 = (bf16[512,640]{1,0:T(8,128)(2,1)}, bf16[512,640]{1,0:T(8,128)(2,1)}, u32[]{:S(2)}, u32[]{:S(2)}) collective-permute-start(bf16[512,640]{1,0:T(8,128)(2,1)} %slice.27), channel_id=1, source_target_pairs={{0,3},{1,0},{2,1},{3,2},{4,7},{5,4},{6,5},{7,6},{8,11},{9,8},{10,9... | collective-permute-start | bytes 1966088 | tf_op jit(solution)/shard_map/ppermute | solution.py:460
  509.4 63.2 %collective-permute-start.1 = (bf16[512,640]{1,0:T(8,128)(2,1)}, bf16[512,640]{1,0:T(8,128)(2,1)}, u32[]{:S(2)}, u32[]{:S(2)}) collective-permute-start(bf16[512,640]{1,0:T(8,128)(2,1)} %slice.24), channel_id=1, source_target_pairs={{0,1},{1,2},{2,3},{3,0},{4,5},{5,6},{6,7},{7,4},{8,9},{9,10},{10,1... | collective-permute-start | bytes 1966088 | tf_op jit(solution)/shard_map/ppermute | solution.py:459
  511.4 61.2 %collective-permute-start.3 = (bf16[512,640]{1,0:T(8,128)(2,1)}, bf16[512,640]{1,0:T(8,128)(2,1)}, u32[]{:S(2)}, u32[]{:S(2)}) collective-permute-start(bf16[512,640]{1,0:T(8,128)(2,1)} %slice.25), channel_id=1, source_target_pairs={{0,3},{1,0},{2,1},{3,2},{4,7},{5,4},{6,5},{7,6},{8,11},{9,8},{10,9... | collective-permute-start | bytes 1966088 | tf_op jit(solution)/shard_map/ppermute | solution.py:460
